TPU v7x, 128 devices: a whole 4x4x4 slice. The times are simulated.
128 devices in a mesh: front: 2 (over core), row: 8 (over y, z_lo), col: 8 (over x, z_hi).
Axes of the slice: x: 4, y: 4, z: 4 (z_hi: 2, z_lo: 2; z = z_hi * 2 + z_lo), core: 2. Of those that a mesh axis runs over, the one named last changes fastest.
Arguments:
- orig_front: float32 [2, 12, 8, 128, 12, 8, 128], P('front', None, 'row', None, None, 'col'), may hold values from -100 to 300, as said below
- child_updates: bfloat16 [2, 2, 8, 8, 128, 8, 8, 128], P('front', None, None, 'row', None, None, 'col'), may hold values from -2 to 2, as said below
- index_maps: int32 [2, 2, 64], replicated, may hold values from 0 to 95, as said below
Outputs:
- factored: float32 [2, 12, 8, 128, 12, 8, 128], P('front', None, 'row', None, None, 'col')
Inputs may be any that keep to these rules, and one draw needn't show every extreme that they name: `index_maps`: within one child, distinct blocks go to distinct parent blocks. Call b mod 8 the grid row of parent block b. Of the 8 child blocks q * 8 + r with one r, at most 2 go to any one grid row and exactly 2 to some; each grid row receives exactly 8 blocks of each child. `orig_front`: each front plus its placed child updates is symmetric, with a positive definite leading block of order 2 * 128. `child_updates`: each child update is symmetric.
All inputs are finite; a program needn't handle non-finite values.
Results may differ from a plain program's by a relative error of at most 0.0003.
Values may be sent and summed in bfloat16 or wider, within the bound.
A program may use at most 128 MiB of HBM per device.

v0:
```python
import jax
import jax.numpy as jnp
from jax import lax
from jax.sharding import Mesh
from jax.sharding import PartitionSpec as P

PANELS = 2
MOST = 2
ROW = ("row_0", "row_1")


def broadcast(value, axis, root):
    return lax.dynamic_index_in_dim(lax.all_gather(value, axis), root, 0, keepdims=False)


def gather_axes(value, axes, dim):
    for axis in reversed(axes):
        value = lax.all_gather(value, axis, axis=dim, tiled=True)
    return value


def earlier_count(target):
    count = target.shape[-1]
    same = target[..., :, None] == target[..., None, :]
    before = (
        jnp.arange(count, dtype=jnp.int32)[None, :] < jnp.arange(count, dtype=jnp.int32)[:, None]
    )
    return jnp.sum(same & before, axis=-1)


def send_table(mapping, mine, grid_size):
    blocks = mapping.shape[-1] // grid_size
    picks = jnp.arange(blocks, dtype=jnp.int32) * grid_size + mine
    target_blocks = jnp.take(mapping, picks, axis=-1)
    target_rows = target_blocks % grid_size
    order = earlier_count(target_rows)
    grid_ids = jnp.arange(grid_size, dtype=jnp.int32)[:, None, None]
    slot_ids = jnp.arange(MOST, dtype=jnp.int32)[None, :, None]
    table = (target_rows[..., None, None, :] == grid_ids) & (order[..., None, None, :] == slot_ids)
    return table.astype(jnp.bfloat16)


def receive_table(mapping, mine, grid_size, parent_blocks):
    blocks = mapping.shape[-1] // grid_size
    by_source = jnp.swapaxes(mapping.reshape(mapping.shape[:-1] + (blocks, grid_size)), -1, -2)
    target_rows = by_source % grid_size
    order = earlier_count(target_rows)
    landing = by_source // grid_size
    arrived = target_rows == mine
    slot_ids = jnp.arange(MOST, dtype=jnp.int32)[:, None, None]
    block_ids = jnp.arange(parent_blocks, dtype=jnp.int32)[None, :, None]
    table = (
        arrived[..., None, None, :]
        & (order[..., None, None, :] == slot_ids)
        & (landing[..., None, None, :] == block_ids)
    )
    return jnp.sum(table.astype(jnp.float32), axis=-1).astype(jnp.bfloat16)


def factor_rows(column, lower, global_ids, step):
    width = column.shape[-1]
    flat = column.reshape(-1, width)
    solved = lax.linalg.triangular_solve(
        lower, flat, left_side=False, lower=True, transpose_a=True
    ).reshape(column.shape)
    placed = jnp.where((global_ids == step)[:, None, None], lower[None], solved)
    return jnp.where((global_ids < step)[:, None, None], jnp.float32(0.0), placed)


def per_device(orig_front, child_updates, index_maps):
    grid_rows = lax.axis_size(ROW)
    grid_cols = lax.axis_size("col")
    my_front = lax.axis_index("front")
    my_row = lax.axis_index(ROW)
    my_col = lax.axis_index("col")
    front_local = orig_front[0, :, 0, :, :, 0, :]
    child_local = child_updates[0, :, :, 0, :, :, 0, :]
    parent_blocks = front_local.shape[0]
    block_size = front_local.shape[1]
    own_maps = lax.dynamic_index_in_dim(index_maps, my_front, 0, keepdims=False)
    children = lax.all_to_all(child_local, "front", split_axis=0, concat_axis=0, tiled=True)
    row_pick = send_table(own_maps, my_row, grid_rows)
    by_rows = jnp.einsum(
        "kdaq,kqxsy->dkaxsy", row_pick, children, preferred_element_type=jnp.float32
    ).astype(jnp.bfloat16)
    row_incoming = lax.all_to_all(by_rows, ROW, split_axis=0, concat_axis=0, tiled=True)
    row_place = receive_table(own_maps, my_row, grid_rows, parent_blocks)
    rows_placed = jnp.einsum(
        "krai,rkaxsy->kixsy", row_place, row_incoming, preferred_element_type=jnp.float32
    ).astype(jnp.bfloat16)
    col_pick = send_table(own_maps, my_col, grid_cols)
    by_cols = jnp.einsum(
        "kebs,kixsy->ekixby", col_pick, rows_placed, preferred_element_type=jnp.float32
    ).astype(jnp.bfloat16)
    col_incoming = lax.all_to_all(by_cols, "col", split_axis=0, concat_axis=0, tiled=True)
    col_place = receive_table(own_maps, my_col, grid_cols, parent_blocks)
    added = jnp.einsum(
        "kcbm,ckixby->ixmy", col_place, col_incoming, preferred_element_type=jnp.float32
    )
    matrix = front_local + added
    rows_global = jnp.arange(parent_blocks, dtype=jnp.int32) * grid_rows + my_row
    cols_global = jnp.arange(parent_blocks, dtype=jnp.int32) * grid_cols + my_col
    for step in range(PANELS):
        owner_row = step % grid_rows
        owner_slot = step // grid_rows
        owner_col = step % grid_cols
        owner_colslot = step // grid_cols
        column = broadcast(matrix[:, :, owner_colslot, :], "col", owner_col)
        whole = gather_axes(column[None], ROW, 0)
        lower = jnp.linalg.cholesky(whole[owner_row, owner_slot])
        all_ids = (
            jnp.arange(parent_blocks, dtype=jnp.int32)[None, :] * grid_rows
            + jnp.arange(grid_rows, dtype=jnp.int32)[:, None]
        ).reshape(-1)
        factor_all = factor_rows(whole.reshape((-1,) + whole.shape[2:]), lower, all_ids, step)
        factor_all = factor_all.reshape(whole.shape)
        factor_mine = lax.dynamic_index_in_dim(factor_all, my_row, 0, keepdims=False)
        factor_other = lax.dynamic_index_in_dim(factor_all, my_col, 0, keepdims=False)
        update = jnp.dot(
            factor_mine.reshape(-1, block_size),
            factor_other.reshape(-1, block_size).T,
            precision=lax.Precision.HIGHEST,
        )
        matrix = matrix - update.reshape(matrix.shape)
        column_hit = (cols_global == step)[None, None, :, None]
        matrix = jnp.where(column_hit, factor_mine[:, :, None, :], matrix)
        row_hit = (rows_global == step)[:, None, None, None] & (cols_global > step)[
            None, None, :, None
        ]
        matrix = jnp.where(row_hit, jnp.float32(0.0), matrix)
    return matrix[None, :, None, :, :, None, :]


def solution(mesh):
    split = Mesh(
        mesh.devices.reshape(mesh.shape["front"], 4, 2, mesh.shape["col"]),
        ("front", "row_0", "row_1", "col"),
    )
    placed = (
        P("front", None, ROW, None, None, "col", None),
        P("front", None, None, ROW, None, None, "col", None),
        P(),
    )
    return jax.shard_map(
        per_device,
        mesh=split,
        in_specs=placed,
        out_specs=P("front", None, ROW, None, None, "col", None),
        check_vma=False,
    )
```

profile of v0, /device:TPU:4, one launch (start us, length us, event | category | flops | bytes accessed | tf_op | source)
XLA Modules:
  0.0 909.7 jit_solution(1990289003103230616)
XLA Ops:
  6.5 9.1 copy.163
  15.6 5.6 all-to-all-start
  21.4 0.6 gather_fusion
  22.1 0.6 gather_fusion.1
  23.1 2.6 all-to-all-done
  25.7 7.9 convert_bitcast_fusion.1
  33.6 8.5 copy.91
  42.1 5.8 all-to-all-start.1
  49.4 114.6 %all-to-all-done.1 = bf16[8,2,2,128,8,128]{5,4,3,2,1,0:T(8,128)(2,1)} async-done(((bf16[8,2,2,128,8,128]{5,4,3,2,1,0:T(8,128)(2,1)}), bf16[8,2,2,128,8,128]{5,4,3,2,1,0:T(8,128)(2,1)}, u32[]{:S(2)}, u32[]{:S(2)}) %all-to-all-start.1) | async-done | bytes 8388640 | tf_op jit(solution)/shard_map/all_to_all | solution.py:86
  164.0 11.0 %fusion.7 = bf16[2,12,128,8,128,1]{4,1,3,2,0,5:T(8,128)(2,1)} fusion(bf16[8,2,2,128,8,128]{5,4,3,2,1,0:T(8,128)(2,1)} %all-to-all-done.1, bf16[2,8,2,12,1,1]{3,2,1,0,5,4:T(2,128)(2,1)S(1)} %bitcast.159), kind=kOutput, calls=%fused_computation.16 | convolution fusion | flops 103809024 | bytes 14680832 | tf_op jit(solution)/shard_map/krai,rkaxsy->kixsy/dot_general | solution.py:88
  175.0 7.0 convert_bitcast_fusion
  182.1 31.3 %copy.98 = bf16[8,2,12,128,2,128]{5,1,4,3,2,0:T(2,128)(2,1)S(1)} copy(bf16[8,2,12,128,2,128]{5,0,1,4,3,2:T(8,128)(2,1)S(1)} %convert_bitcast_fusion) | data formatting | bytes 25165824 | tf_op jit(solution)/shard_map/convert_element_type | solution.py:94
  213.4 145.6 %all_to_all.15 = bf16[8,2,12,128,2,128]{5,1,4,3,2,0:T(2,128)(2,1)} all-to-all(bf16[8,2,12,128,2,128]{5,1,4,3,2,0:T(2,128)(2,1)S(1)} %copy.98), channel_id=1, replica_groups=mesh['front'=2,'row_0'=4,'row_1'=2,'col'=8] {'col'}, dimensions={0} | all-to-all | bytes 25165824 | tf_op jit(solution)/shard_map/all_to_all | solution.py:95
  359.0 20.1 %bitcast_add_fusion = f32[12,128,12,128]{3,2,1,0:T(8,128)} fusion(f32[1,12,1,128,12,1,128]{6,5,4,3,2,1,0:T(1,128)} %param.8, bf16[8,2,12,128,2,128]{5,1,4,3,2,0:T(2,128)(2,1)} %all_to_all.15, bf16[2,8,2,12,1,1]{3,2,1,0,5,4:T(2,128)(2,1)S(1)} %bitcast.158), kind=kOutput, calls=%fused_computation.5 | convolution fusion | flops 153354240 | bytes 31458048 | tf_op jit(solution)/shard_map/kcbm,ckixby->ixmy/dot_general | solution.py:97
  379.1 4.1 slice.30
  383.3 85.5 %all-gather.15.cloned.1.call-done = f32[96,128,1,128]{3,1,2,0:T(8,128)} async-done(((f32[12,128,1,128]{3,1,2,0:T(8,128)}), f32[96,128,1,128]{3,1,2,0:T(8,128)}) %all-gather.15.cloned.1.call-update) | async-done | bytes 6291472 | tf_op jit(solution)/shard_map/all_gather | solution.py:13
  468.8 2.1 slice.31
  470.9 29.1 %all-gather.19.cloned.1.call-done = f32[24,128,1,128]{3,1,2,0:T(8,128)} async-done(((f32[12,128,1,128]{3,1,2,0:T(8,128)}), f32[24,128,1,128]{3,1,2,0:T(8,128)}) %all-gather.19.cloned.1.call-update) | async-done | bytes 1572880 | tf_op jit(solution)/shard_map/all_gather | solution.py:18
  500.7 67.7 %all-gather.11.cloned.1.call-done = f32[8,12,128,128]{3,2,1,0:T(8,128)} async-done(((f32[2,12,128,128]{3,2,1,0:T(8,128)}), f32[8,12,128,128]{3,2,1,0:T(8,128)}) %all-gather.11.cloned.1.call-update) | async-done | bytes 6291472 | tf_op jit(solution)/shard_map/all_gather | solution.py:18
  568.3 0.8 slice.32
  569.3 0.9 fusion.27
  570.1 11.7 %cholesky.44 = f32[128,128]{1,0:T(8,128)S(1)} custom-call(f32[128,128]{1,0:T(8,128)S(1)} %fusion.27), custom_call_target="Cholesky" | custom-call | tf_op jit(solution)/shard_map/jit(cholesky)/cholesky | solution.py:110
  581.9 0.6 compare_reduce_fusion.1
  582.5 0.7 fusion.34
  583.2 9.8 %custom-call.6 = f32[1,128,128]{1,2,0:T(8,128)S(1)} custom-call(f32[1,128,128]{2,1,0:T(8,128)S(1)} %get-tuple-element.14), custom_call_target="InvertDiagBlocksLowerTriangular" | custom-call | tf_op jit(solution)/shard_map/triangular_solve/custom-call.0 | solution.py:63
  593.0 9.6 %convolution_bitcast_fusion.1 = f32[12288,128]{0,1:T(8,128)} fusion(f32[12288,128]{1,0:T(8,128)} %bitcast.152, f32[1,128,128]{1,2,0:T(8,128)S(1)} %custom-call.6), kind=kOutput, calls=%fused_computation.4 | convolution fusion | flops 2415919104 | bytes 12648448 | tf_op jit(solution)/shard_map/triangular_solve/dot.4 | solution.py:63
  602.6 6.5 copy.106
  609.1 3.4 select_select_fusion.1
  612.6 9.9 %fusion.18 = f32[12,128,12,128]{3,1,2,0:T(8,128)} fusion(f32[8,12,128,128]{3,2,1,0:T(8,128)S(1)} %select_select_fusion.1, s32[]{:T(128)S(6)} %select_n.91, s32[]{:T(128)S(6)} %select_n.90), kind=kOutput, calls=%fused_computation.27 | convolution fusion | flops 3623878656 | bytes 11010056 | tf_op jit(solution)/shard_map/dot_general | solution.py:119
  622.5 10.6 %fusion.4 = f32[12,128,12,128]{3,2,1,0:T(8,128)S(1)} fusion(f32[12,128,12,128]{3,2,1,0:T(8,128)S(1)} %bitcast.146, f32[12,128,12,128]{3,1,2,0:T(8,128)} %fusion.18, f32[12,128,128]{2,1,0:T(8,128)S(1)} %dynamic-slice_bitcast_fusion.1, pred[12]{0:T(512)(128)(4,1)S(1)} %get-tuple-element.29, pred[12,12]{1,0:T(8,128)(4,1)S(1)} %broadcast_and_fusion), kind=kLoop, calls=%fused_computation.12 | loop fusion | flops 7077888 | bytes 29098140 | tf_op jit(solution)/shard_map/jit(_where)/select_n | solution.py:130
  633.1 4.5 copy-done.2
  637.6 1.3 slice.33
  639.0 88.4 %all-gather.17.cloned.1.call-done = f32[96,128,1,128]{3,1,2,0:T(8,128)} async-done(((f32[12,128,1,128]{3,1,2,0:T(8,128)}), f32[96,128,1,128]{3,1,2,0:T(8,128)}) %all-gather.17.cloned.1.call-update) | async-done | bytes 6291472 | tf_op jit(solution)/shard_map/all_gather | solution.py:13
  727.4 2.1 slice.34
  729.8 28.9 %all-gather.21.cloned.1.call-done = f32[24,128,1,128]{3,1,2,0:T(8,128)} async-done(((f32[12,128,1,128]{3,1,2,0:T(8,128)}), f32[24,128,1,128]{3,1,2,0:T(8,128)}) %all-gather.21.cloned.1.call-update) | async-done | bytes 1572880 | tf_op jit(solution)/shard_map/all_gather | solution.py:18
  758.7 68.1 %all-gather.13.cloned.1.call-done = f32[8,12,128,128]{3,2,1,0:T(8,128)} async-done(((f32[2,12,128,128]{3,2,1,0:T(8,128)}), f32[8,12,128,128]{3,2,1,0:T(8,128)}) %all-gather.13.cloned.1.call-update) | async-done | bytes 6291472 | tf_op jit(solution)/shard_map/all_gather | solution.py:18
  826.8 0.8 slice.35
  827.7 0.9 fusion.26
  828.6 11.7 %cholesky.55 = f32[128,128]{1,0:T(8,128)S(1)} custom-call(f32[128,128]{1,0:T(8,128)S(1)} %fusion.26), custom_call_target="Cholesky" | custom-call | tf_op jit(solution)/shard_map/jit(cholesky)/cholesky | solution.py:110
  840.3 0.6 compare_reduce_fusion
  841.0 0.7 select_bitcast_fusion
  841.6 9.8 %custom-call.7 = f32[1,128,128]{1,2,0:T(8,128)S(1)} custom-call(f32[1,128,128]{2,1,0:T(8,128)S(1)} %get-tuple-element.12), custom_call_target="InvertDiagBlocksLowerTriangular" | custom-call | tf_op jit(solution)/shard_map/triangular_solve/custom-call.0 | solution.py:63
  851.5 9.4 %convolution_bitcast_fusion = f32[12288,128]{0,1:T(8,128)} fusion(f32[12288,128]{1,0:T(8,128)} %bitcast.153, f32[1,128,128]{1,2,0:T(8,128)S(1)} %custom-call.7), kind=kOutput, calls=%fused_computation.3 | convolution fusion | flops 2415919104 | bytes 12648448 | tf_op jit(solution)/shard_map/triangular_solve/dot.4 | solution.py:63
  860.9 6.5 copy.111
  867.4 3.4 select_select_fusion
  870.8 9.9 %fusion.16 = f32[12,128,12,128]{3,1,2,0:T(8,128)} fusion(f32[8,12,128,128]{3,2,1,0:T(8,128)S(1)} %select_select_fusion, s32[]{:T(128)S(6)} %select_n.91, s32[]{:T(128)S(6)} %select_n.90), kind=kOutput, calls=%fused_computation.25 | convolution fusion | flops 3623878656 | bytes 11010056 | tf_op jit(solution)/shard_map/dot_general | solution.py:119
  880.8 10.6 %fusion.2 = f32[1,12,1,128,12,1,128]{6,4,3,1,5,2,0:T(8,128)S(1)} fusion(f32[12,128,12,128]{3,2,1,0:T(8,128)S(1)} %bitcast.148, f32[12,128,12,128]{3,1,2,0:T(8,128)} %fusion.16, f32[12,128,128]{2,1,0:T(8,128)S(1)} %dynamic-slice_bitcast_fusion, pred[12]{0:T(512)(128)(4,1)S(1)} %get-tuple-element.31, pred[12,12]{1,0:T(8,128)(4,1)S(1)} %broadcast_and_fusion.1), kind=kLoop, calls=%fused_computation.9 | loop fusion | flops 7077888 | bytes 29098140 | tf_op jit(solution)/shard_map/broadcast_in_dim | solution.py:131
  891.4 11.1 %copy.113 = f32[1,12,1,128,12,1,128]{6,5,4,3,2,1,0:T(1,128)} copy(f32[1,12,1,128,12,1,128]{6,4,3,1,5,2,0:T(8,128)S(1)} %fusion.2) | data formatting | bytes 18874368 | tf_op jit(solution)/shard_map/broadcast_in_dim | solution.py:131
  (73 shorter events, 3.7 us)
Async XLA Ops:
  6.5 14.7 %copy-start = (s32[2,2,64]{2,1,0:T(2,128)S(1)}, s32[2,2,64]{2,1,0:T(2,128)}, u32[]{:S(2)}) copy-start(s32[2,2,64]{2,1,0:T(2,128)} %param.10) | copy-start | bytes 3076
  15.6 10.1 %all-to-all-start = ((bf16[2,8,128,8,128]{4,1,3,2,0:T(8,128)(2,1)}), bf16[2,8,128,8,128]{4,1,3,2,0:T(8,128)(2,1)}, u32[]{:S(2)}, u32[]{:S(2)}) async-start(bf16[2,8,128,8,128]{4,1,3,2,0:T(8,128)(2,1)} %bitcast.151), calls=%async_computation | async-start | bytes 8388608 | tf_op jit(solution)/shard_map/all_to_all | solution.py:81
  42.1 121.9 %all-to-all-start.1 = ((bf16[8,2,2,128,8,128]{5,4,3,2,1,0:T(8,128)(2,1)}), bf16[8,2,2,128,8,128]{5,4,3,2,1,0:T(8,128)(2,1)}, u32[]{:S(2)}, u32[]{:S(2)}) async-start(bf16[8,2,2,128,8,128]{5,4,3,2,1,0:T(8,128)(2,1)} %copy.91), calls=%async_computation.1 | async-start | bytes 16777216 | tf_op jit(solution)/shard_map/all_to_all | solution.py:86
  47.9 420.8 %all-gather.15.cloned.1.call-start = ((), (), s32[]{:S(2)}) async-start(), calls=%async_computation.5 | async-start | bytes 7077888 | tf_op jit(solution)/shard_map/all_gather | solution.py:13
  383.2 116.8 %all-gather.19.cloned.1.call-start = ((), (), s32[]{:S(2)}) async-start(), calls=%async_computation.7 | async-start | bytes 2359296 | tf_op jit(solution)/shard_map/all_gather | solution.py:18
  470.9 97.5 %all-gather.11.cloned.1.call-start = ((), (), s32[]{:S(2)}) async-start(), calls=%async_computation.3 | async-start | bytes 7864320 | tf_op jit(solution)/shard_map/all_gather | solution.py:18
  500.0 227.4 %all-gather.17.cloned.1.call-start = ((), (), s32[]{:S(2)}) async-start(), calls=%async_computation.6 | async-start | bytes 7077888 | tf_op jit(solution)/shard_map/all_gather | solution.py:13
  609.1 13.4 %slice-start = ((s8[12582912]{0:T(1024)(128)(4,1)}), s8[4194304]{0:T(1024)(128)(4,1)S(1)}, s32[]{:S(2)}) async-start(s8[12582912]{0:T(1024)(128)(4,1)} %bitcast.145), calls=%async_computation.9 | async-start | bytes 8388608
  609.1 13.4 %slice-start.1 = ((s8[12582912]{0:T(1024)(128)(4,1)}), s8[4194304]{0:T(1024)(128)(4,1)S(1)}, s32[]{:S(2)}) async-start(s8[12582912]{0:T(1024)(128)(4,1)} %bitcast.145), calls=%async_computation.10 | async-start | bytes 8388608
  612.6 9.9 %slice-start.2 = ((s8[12582912]{0:T(1024)(128)(4,1)}), s8[4194304]{0:T(1024)(128)(4,1)S(1)}, s32[]{:S(2)}) async-start(s8[12582912]{0:T(1024)(128)(4,1)} %bitcast.145), calls=%async_computation.11 | async-start | bytes 8388608
  633.1 4.5 copy-start.2
  639.0 119.7 %all-gather.21.cloned.1.call-start = ((), (), s32[]{:S(2)}) async-start(), calls=%async_computation.8 | async-start | bytes 2359296 | tf_op jit(solution)/shard_map/all_gather | solution.py:18
  729.5 97.3 %all-gather.13.cloned.1.call-start = ((), (), s32[]{:S(2)}) async-start(), calls=%async_computation.4 | async-start | bytes 7864320 | tf_op jit(solution)/shard_map/all_gather | solution.py:18
  867.4 13.4 %slice-start.3 = ((s8[12582912]{0:T(1024)(128)(4,1)}), s8[4194304]{0:T(1024)(128)(4,1)S(1)}, s32[]{:S(2)}) async-start(s8[12582912]{0:T(1024)(128)(4,1)} %bitcast.147), calls=%async_computation.12 | async-start | bytes 8388608
  867.4 13.4 %slice-start.4 = ((s8[12582912]{0:T(1024)(128)(4,1)}), s8[4194304]{0:T(1024)(128)(4,1)S(1)}, s32[]{:S(2)}) async-start(s8[12582912]{0:T(1024)(128)(4,1)} %bitcast.147), calls=%async_computation.13 | async-start | bytes 8388608
  870.8 10.0 %slice-start.5 = ((s8[12582912]{0:T(1024)(128)(4,1)}), s8[4194304]{0:T(1024)(128)(4,1)S(1)}, s32[]{:S(2)}) async-start(s8[12582912]{0:T(1024)(128)(4,1)} %bitcast.147), calls=%async_computation.14 | async-start | bytes 8388608
  880.8 21.7 %copy-start.1 = (s32[2,2,64]{2,1,0:T(2,128)S(1)}, s32[2,2,64]{2,1,0:T(2,128)}, u32[]{:S(2)}) copy-start(s32[2,2,64]{2,1,0:T(2,128)} %param.10) | copy-start | bytes 3076
Sparse Core Ops, SparseCore 0:
  383.4 85.3 all-gather.14
  471.0 28.9 all-gather.18
  501.7 66.6 all-gather.10
  639.1 88.2 all-gather.16
  729.6 28.9 all-gather.20
  760.1 66.6 all-gather.12
where the time goes:
time: 918 us; the launch traced here: 910 us
  waiting for transfers between devices  485 us (53%)
  blocking collectives  146 us (16%)
  local copies, waits for them, and re-layouts  90.9 us (10%)
  matrix products  84.9 us (9%)
  other arithmetic  76.7 us (8%)
  between operations  14.2 us (2%)
  starting transfers between devices  12.5 us (1%)
    all_gather x4, waiting for transfers between devices, gather_axes(): value = lax.all_gather(value, axis, axis=dim, tiled=True)  194 us
    all_gather x2, waiting for transfers between devices, broadcast(): lax.all_gather(value, axis)  174 us
    all_to_all x1, blocking collectives, per_device(): lax.all_to_all(by_cols, 'col', split_axis=0, concat_axis=0, tiled=True)  146 us
    all_to_all x1, waiting for transfers between devices, per_device(): lax.all_to_all(by_rows, ROW, split_axis=0, concat_axis=0, tiled=True)  115 us
    convert_element_type x1, local copies, waits for them, and re-layouts, per_device(): by_cols = jnp.einsum('kebs,kixsy->ekixby', col_pick, rows_placed, preferr...  31.3 us
    another operation x6, other arithmetic, per_device(): lower = jnp.linalg.cholesky(whole[owner_row, owner_slot])  24.8 us
    another operation x4, other arithmetic, factor_rows(): lax.linalg.triangular_solve(lower, flat, left_side=False, lower=True, tra...  20.9 us
    dot_general x1, matrix products, per_device(): jnp.einsum('kcbm,ckixby->ixmy', col_place, col_incoming, preferred_elemen...  20.1 us
  transfers between devices with their start and end apart: 8, of which 8 were waited for; matrix products, arithmetic and copies ran while one was open for 0% of the time, Pallas kernels for 0%

commit v1 on v0

v1 whole, which is shorter than its diff:
```python
import functools

import jax
import jax.numpy as jnp
from jax import lax
from jax.experimental import pallas as pl
from jax.experimental.pallas import tpu as pltpu
from jax.sharding import PartitionSpec as P

F32 = jnp.float32
BF16 = jnp.bfloat16
I32 = jnp.int32
MESH = pl.DeviceIdType.MESH
HIGHEST = lax.Precision.HIGHEST
HBM = pltpu.MemorySpace.HBM
VMEM = pltpu.MemorySpace.VMEM
SMEM = pltpu.MemorySpace.SMEM


def tables(maps, front, row, col, grid, parent_blocks):
    blocks = maps.shape[-1] // grid
    by_source = maps.reshape(2, 2, blocks, grid)
    target = by_source % grid
    place = by_source // grid
    ids = jnp.arange(blocks, dtype=I32)
    before = ids[None, :] < ids[:, None]
    same = target[:, :, :, None, :] == target[:, :, None, :, :]
    order = jnp.sum((same & before[None, None, :, :, None]).astype(I32), axis=3)
    send_slot = target * 2 + order
    recv_slot = jnp.arange(grid, dtype=I32) * 2 + order
    mine = lax.dynamic_index_in_dim(by_source, front, 1, keepdims=False)
    row_send = lax.dynamic_index_in_dim(
        lax.dynamic_index_in_dim(send_slot, front, 1, keepdims=False), row, 2, keepdims=False
    )
    held_rows = lax.dynamic_index_in_dim(mine, row, 2, keepdims=False)
    held_cols = lax.dynamic_index_in_dim(mine, col, 2, keepdims=False)
    lead = jnp.arange(2, dtype=I32)
    lead_row = jnp.sum(
        (held_rows[:, None, :] == lead[None, :, None]).astype(I32) * (ids + 1), axis=-1
    ) - 1
    lead_col = jnp.sum(
        (held_cols[:, None, :] == lead[None, :, None]).astype(I32) * (ids + 1), axis=-1
    ) - 1
    own = lambda value: lax.dynamic_index_in_dim(value, front, 0, keepdims=False)
    own_target, own_place, own_recv = own(target), own(place), own(recv_slot)
    col_send = lax.dynamic_index_in_dim(own(send_slot), col, 2, keepdims=False)
    flat = lambda value: value.reshape(2, blocks * grid)
    row_hit = flat(own_target == row).astype(I32)
    col_hit = flat(own_target == col).astype(I32)
    count = jnp.arange(blocks * grid, dtype=I32)
    rank = jnp.sum(row_hit[:, None, :] * (count[None, :] < count[:, None]).astype(I32), axis=-1)
    row_slot = jnp.sum(
        row_hit[:, None, :] * (rank[:, None, :] == ids[None, :, None]).astype(I32) * flat(own_recv)[:, None, :],
        axis=-1,
    )
    spots = jnp.arange(parent_blocks, dtype=I32)
    at = (flat(own_place)[:, None, :] == spots[None, :, None]).astype(I32)
    row_pos = jnp.sum(row_hit[:, None, :] * at * (rank + 1)[:, None, :], axis=-1) - 1
    col_pos = jnp.sum(col_hit[:, None, :] * at * (flat(own_recv) + 1)[:, None, :], axis=-1) - 1
    return row_send, lead_row, lead_col, row_slot, col_send, row_pos, col_pos


def pack_rows_kernel(slot_ref, lrow_ref, lcol_ref, where_ref, child_ref, corner_ref, out_ref, lead_ref, wide):
    p, q = pl.program_id(0), pl.program_id(1)
    size, blocks = child_ref.shape[2], child_ref.shape[3]
    wide[...] = child_ref[0, 0].astype(F32).reshape(size * blocks, size)

    @pl.when(q == 0)
    def _():
        for a in range(2):
            for b in range(2):
                hit = (where_ref[0] == p) & (where_ref[1] == a) & (where_ref[2] == b)
                lead_ref[0, a, b] = jnp.where(hit, corner_ref[...], 0.0)

    for j in range(blocks):
        out_ref[0, 0, j] = wide[pl.ds(j, size, stride=blocks), :].astype(BF16)

    for a in range(2):
        for b in range(2):

            @pl.when((lrow_ref[2 * p + a] == q) & (lcol_ref[2 * p + b] >= 0))
            def _():
                j = jnp.maximum(lcol_ref[2 * p + b], 0)
                lead_ref[0, a, b] = lead_ref[0, a, b] + out_ref[0, 0, j].astype(F32)


def pack_rows(child, corner, slots, lead_row, lead_col, where, grid):
    _, blocks, size, _, _ = child.shape
    return pl.pallas_call(
        pack_rows_kernel,
        grid_spec=pltpu.PrefetchScalarGridSpec(
            num_scalar_prefetch=4,
            grid=(2, blocks),
            in_specs=[
                pl.BlockSpec((1, 1, size, blocks, size), lambda p, q, *_: (p, q, 0, 0, 0)),
                pl.BlockSpec((size, size), lambda p, q, *_: (0, 0)),
            ],
            out_specs=[
                pl.BlockSpec((1, 1, blocks, size, size), lambda p, q, s, *_: (p, s[p * blocks + q], 0, 0, 0)),
                pl.BlockSpec((1, 2, 2, size, size), lambda p, q, *_: (p, 0, 0, 0, 0)),
            ],
            scratch_shapes=[pltpu.VMEM((size * blocks, size), F32)],
        ),
        out_shape=[
            jax.ShapeDtypeStruct((2, grid * 2, blocks, size, size), BF16),
            jax.ShapeDtypeStruct((2, 2, 2, size, size), F32),
        ],
        compiler_params=pltpu.CompilerParams(dimension_semantics=("arbitrary", "arbitrary")),
        cost_estimate=pl.CostEstimate(flops=2_000_000, bytes_accessed=4 * child.size, transcendentals=0),
        name="pack_rows",
    )(slots.reshape(-1), lead_row.reshape(-1), lead_col.reshape(-1), where, child, corner)


def pack_cols_kernel(row_ref, slot_ref, in_ref, out_ref):
    k = pl.program_id(0)
    blocks = in_ref.shape[2]
    for j in range(blocks):
        out_ref[0, 0, slot_ref[k * blocks + j]] = in_ref[0, 0, j]


def pack_cols(received, row_slot, col_send, grid):
    _, _, blocks, size, _ = received.shape
    return pl.pallas_call(
        pack_cols_kernel,
        grid_spec=pltpu.PrefetchScalarGridSpec(
            num_scalar_prefetch=2,
            grid=(2, blocks),
            in_specs=[
                pl.BlockSpec((1, 1, blocks, size, size), lambda k, j, r, *_: (k, r[k * blocks + j], 0, 0, 0))
            ],
            out_specs=pl.BlockSpec((1, 1, grid * 2, size, size), lambda k, j, *_: (k, j, 0, 0, 0)),
        ),
        out_shape=jax.ShapeDtypeStruct((2, blocks, grid * 2, size, size), BF16),
        compiler_params=pltpu.CompilerParams(dimension_semantics=("arbitrary", "arbitrary")),
        cost_estimate=pl.CostEstimate(flops=2_000_000, bytes_accessed=4 * received.size, transcendentals=0),
        name="pack_cols",
    )(row_slot.reshape(-1), col_send.reshape(-1), received)


def meet(peers):
    barrier = pltpu.get_barrier_semaphore()
    for peer in peers:
        pl.semaphore_signal(barrier, inc=1, device_id=peer, device_id_type=MESH)
    pl.semaphore_wait(barrier, len(peers))


def hop_order(grid):
    return [d for pair in zip(range(1, grid), range(grid - 1, 0, -1)) for d in pair][: grid - 1]


def row_exchange_kernel(grid, send_ref, recv_ref, send_sem, recv_sem, local_sem):
    f, r, c = lax.axis_index("front"), lax.axis_index("row"), lax.axis_index("col")
    others = [(p, d) for d in hop_order(grid) for p in range(2)] + [(1, 0)]
    peers = [(lax.rem(f + p, 2), lax.rem(r + d, grid), c) for p, d in others]
    local = pltpu.make_async_copy(send_ref.at[f, pl.ds(2 * r, 2)], recv_ref.at[f, pl.ds(2 * r, 2)], local_sem)
    local.start()
    meet(peers)
    copies = []
    for n, (p, d) in enumerate(others):
        peer = peers[n]
        copy = pltpu.make_async_remote_copy(
            src_ref=send_ref.at[peer[0], pl.ds(2 * peer[1], 2)],
            dst_ref=recv_ref.at[f, pl.ds(2 * r, 2)],
            send_sem=send_sem.at[n],
            recv_sem=recv_sem.at[p, d],
            device_id=peer,
            device_id_type=MESH,
        )
        copy.start()
        copies.append(copy)
    local.wait()
    for copy in copies:
        copy.wait_send()
    for copy in copies:
        copy.wait_recv()


def row_exchange(packed, grid):
    n = 2 * grid
    return pl.pallas_call(
        functools.partial(row_exchange_kernel, grid),
        out_shape=jax.ShapeDtypeStruct(packed.shape, BF16),
        in_specs=[pl.BlockSpec(memory_space=HBM)],
        out_specs=pl.BlockSpec(memory_space=HBM),
        scratch_shapes=[
            pltpu.SemaphoreType.DMA((n,)),
            pltpu.SemaphoreType.DMA((2, grid)),
            pltpu.SemaphoreType.DMA,
        ],
        compiler_params=pltpu.CompilerParams(collective_id=1, has_side_effects=True),
        cost_estimate=pl.CostEstimate(flops=100_000_000, bytes_accessed=4 * packed.size, transcendentals=0),
        name="row_exchange",
    )(packed)


def factor_block(work, size):
    lanes = lax.broadcasted_iota(I32, (size, size), 1)
    rows = lax.broadcasted_iota(I32, (size, 1), 0)

    def step(j, carry):
        pivot_row = work[pl.ds(j, 1), :]
        left = work[:, :size]
        column = jnp.sum(jnp.where(lanes == j, left, 0.0), axis=1, keepdims=True)
        pivot = jnp.sum(jnp.where(lanes[:1] == j, pivot_row[:, :size], 0.0), axis=1, keepdims=True)
        scale = jnp.where(rows > j, column / pivot, 0.0)
        work[...] = work[...] - scale * pivot_row
        return carry

    lax.fori_loop(0, size, step, 0)


def triangular(work, size):
    eye = lax.broadcasted_iota(I32, (size, size), 0) == lax.broadcasted_iota(I32, (size, size), 1)
    upper = lax.broadcasted_iota(I32, (size, size), 0) <= lax.broadcasted_iota(I32, (size, size), 1)
    u = work[:, :size]
    root = lax.rsqrt(jnp.sum(jnp.where(eye, u, 0.0), axis=1, keepdims=True))
    lower = jnp.where(upper, u * root, 0.0).T
    inverse = work[:, size:] * root
    return lower, inverse


def mm(a, b):
    return jnp.dot(a, b, precision=HIGHEST, preferred_element_type=F32)


def mm_t(a, b):
    return lax.dot_general(a, b, (((1,), (1,)), ((), ())), precision=HIGHEST, preferred_element_type=F32)


def factor_lead(lead_ref, low_ref, inv_ref, work, size):
    eye = (
        lax.broadcasted_iota(I32, (size, size), 0) == lax.broadcasted_iota(I32, (size, size), 1)
    ).astype(F32)
    work[:, :size] = lead_ref[0, 0]
    work[:, size:] = eye
    factor_block(work, size)
    l0, i0 = triangular(work, size)
    l10 = mm_t(lead_ref[1, 0], i0)
    work[:, :size] = lead_ref[1, 1] - mm_t(l10, l10)
    work[:, size:] = eye
    factor_block(work, size)
    l1, i1 = triangular(work, size)
    low_ref[0] = jnp.concatenate([l0, jnp.zeros_like(l0)], axis=1)
    low_ref[1] = jnp.concatenate([l10, l1], axis=1)
    inv_ref[:size, :size] = i0
    inv_ref[:size, size:] = jnp.zeros_like(i0)
    inv_ref[size:, :size] = -mm(i1, mm(l10, i0))
    inv_ref[size:, size:] = i1


def col_exchange_kernel(grid, size, send_ref, lead_ref, recv_ref, low_ref, inv_ref, work, send_sem, recv_sem, local_sem):
    f, r, c = lax.axis_index("front"), lax.axis_index("row"), lax.axis_index("col")
    others = hop_order(grid)
    peers = [(f, r, lax.rem(c + d, grid)) for d in others]
    local = pltpu.make_async_copy(send_ref.at[:, :, pl.ds(2 * c, 2)], recv_ref.at[c], local_sem)
    local.start()
    meet(peers)
    copies = []
    for n, d in enumerate(others):
        copy = pltpu.make_async_remote_copy(
            src_ref=send_ref.at[:, :, pl.ds(2 * peers[n][2], 2)],
            dst_ref=recv_ref.at[c],
            send_sem=send_sem.at[n],
            recv_sem=recv_sem.at[d],
            device_id=peers[n],
            device_id_type=MESH,
        )
        copy.start()
        copies.append(copy)
    factor_lead(lead_ref, low_ref, inv_ref, work, size)
    local.wait()
    for copy in copies:
        copy.wait_send()
    for copy in copies:
        copy.wait_recv()


def col_exchange(packed, lead, grid):
    _, blocks, _, size, _ = packed.shape
    return pl.pallas_call(
        functools.partial(col_exchange_kernel, grid, size),
        out_shape=[
            jax.ShapeDtypeStruct((grid, 2, blocks, 2, size, size), BF16),
            jax.ShapeDtypeStruct((2, size, 2 * size), F32),
            jax.ShapeDtypeStruct((2 * size, 2 * size), F32),
        ],
        in_specs=[pl.BlockSpec(memory_space=HBM), pl.BlockSpec(memory_space=VMEM)],
        out_specs=[
            pl.BlockSpec(memory_space=HBM),
            pl.BlockSpec(memory_space=VMEM),
            pl.BlockSpec(memory_space=VMEM),
        ],
        scratch_shapes=[
            pltpu.VMEM((size, 2 * size), F32),
            pltpu.SemaphoreType.DMA((grid,)),
            pltpu.SemaphoreType.DMA((grid,)),
            pltpu.SemaphoreType.DMA,
        ],
        compiler_params=pltpu.CompilerParams(collective_id=2, has_side_effects=True),
        cost_estimate=pl.CostEstimate(flops=100_000_000, bytes_accessed=4 * packed.size, transcendentals=0),
        name="col_exchange",
    )(packed, lead)


def added(base, parts):
    for ref, index, valid in parts:
        base = base + jnp.where(valid, ref(jnp.maximum(index, 0)).astype(F32), 0.0)
    return base


def panel_kernel(spots, row_ref, col_ref, fcol_ref, frow_ref, c0, c1, r0, r1, rows_out, cols_out):
    size = fcol_ref.shape[-1]
    cols = (c0, c1)
    rows = (r0, r1)
    for l in range(spots):
        parts = []
        for k in range(2):
            index = row_ref[k * spots + l]
            valid = (index >= 0) & (col_ref[k * spots] >= 0)
            parts.append((lambda i, k=k: cols[k][0, 0, i, 0], index, valid))
        rows_out[l] = added(fcol_ref[l], parts)
        parts = []
        for k in range(2):
            index = col_ref[k * spots + l]
            valid = (index >= 0) & (row_ref[k * spots] >= 0)
            parts.append((lambda i, k=k: rows[k][i // 2, 0, 0, i % 2], index, valid))
        cols_out[l] = added(frow_ref[pl.ds(l, size, stride=spots), :], parts).T


def panels(received, fcol, flat, row_pos, col_pos):
    grid, _, blocks, _, size, _ = received.shape
    spots = fcol.shape[0]

    def by_col(k):
        def index(_, row, col):
            i = jnp.maximum(col[k * spots], 0)
            return (i // 2, k, 0, i % 2, 0, 0)

        return pl.BlockSpec((1, 1, blocks, 1, size, size), index)

    def by_row(k):
        return pl.BlockSpec(
            (grid, 1, 1, 2, size, size),
            lambda _, row, col: (0, k, jnp.maximum(row[k * spots], 0), 0, 0, 0),
        )

    shape = jax.ShapeDtypeStruct((spots, size, size), F32)
    whole = pl.BlockSpec((spots, size, size), lambda *_: (0, 0, 0))
    return pl.pallas_call(
        functools.partial(panel_kernel, spots),
        grid_spec=pltpu.PrefetchScalarGridSpec(
            num_scalar_prefetch=2,
            grid=(1,),
            in_specs=[
                whole,
                pl.BlockSpec((size * spots, size), lambda *_: (0, 0)),
                by_col(0),
                by_col(1),
                by_row(0),
                by_row(1),
            ],
            out_specs=[whole, whole],
        ),
        out_shape=[shape, shape],
        cost_estimate=pl.CostEstimate(flops=2_000_000, bytes_accessed=6_000_000, transcendentals=0),
        name="panels",
    )(row_pos.reshape(-1), col_pos.reshape(-1), fcol, flat, received, received, received, received)


def spread_kernel(grid, spots, rows_ref, cols_ref, rows_out, cols_out, one_send, one_recv, two_send, two_recv):
    f, r, c = lax.axis_index("front"), lax.axis_index("row"), lax.axis_index("col")
    half = grid // 2
    part = spots // half
    row_peer = lambda i: (f, r, i)
    col_peer = lambda i: (f, i, c)
    groups = ((rows_ref, rows_out, c, row_peer), (cols_ref, cols_out, r, col_peer))
    meet([peer(lax.rem(me + d, grid)) for _, _, me, peer in groups for d in range(1, grid)])

    def first(g, s, n):
        source, out, me, peer = groups[g]
        to = lax.rem(s + n, grid)
        piece = pl.ds((to // 2) * part, part)
        return pltpu.make_async_remote_copy(
            src_ref=source.at[piece],
            dst_ref=out.at[s, piece],
            send_sem=one_send.at[g, n],
            recv_sem=one_recv.at[g, s],
            device_id=peer(to),
            device_id_type=MESH,
        )

    def second(g, s, n, source):
        _, out, me, peer = groups[g]
        piece = pl.ds((me // 2) * part, part)
        return pltpu.make_async_remote_copy(
            src_ref=source.at[piece],
            dst_ref=out.at[s, piece],
            send_sem=two_send.at[g, s, n],
            recv_sem=two_recv.at[g, s, n],
            device_id=peer(lax.rem(me + 2 * n, grid)),
            device_id_type=MESH,
        )

    for g in range(2):
        for s in range(2):

            @pl.when(groups[g][2] == s)
            def _():
                for n in hop_order(grid):
                    first(g, s, n).start()

    for g in range(2):
        source, out, me, _ = groups[g]
        for s in range(2):

            @pl.when(me == s)
            def _():
                out[s, pl.ds(0, part)] = source[pl.ds(0, part)]
                for n in range(1, half):
                    second(g, s, n, source).start()

    for g in range(2):
        _, out, me, _ = groups[g]
        for s in range(2):

            @pl.when(me != s)
            def _():
                piece = pl.ds((me // 2) * part, part)
                pltpu.make_async_remote_copy(
                    src_ref=out.at[s, piece],
                    dst_ref=out.at[s, piece],
                    send_sem=one_send.at[g, 0],
                    recv_sem=one_recv.at[g, s],
                    device_id=groups[g][3](s),
                    device_id_type=MESH,
                ).wait_recv()
                for n in range(1, half):
                    second(g, s, n, out.at[s]).start()

    for g in range(2):
        source, out, me, _ = groups[g]
        for s in range(2):

            @pl.when(me == s)
            def _():
                for n in hop_order(grid):
                    first(g, s, n).wait_send()

            for n in range(1, half):
                second(g, s, n, out.at[s]).wait_send()
                piece = pl.ds(lax.rem(me // 2 + half - n, half) * part, part)
                pltpu.make_async_remote_copy(
                    src_ref=out.at[s, piece],
                    dst_ref=out.at[s, piece],
                    send_sem=two_send.at[g, s, n],
                    recv_sem=two_recv.at[g, s, n],
                    device_id=groups[g][3](lax.rem(me + 2 * n, grid)),
                    device_id_type=MESH,
                ).wait_recv()


def spread(rows, cols, grid):
    spots, size, _ = rows.shape
    half = grid // 2
    shape = jax.ShapeDtypeStruct((2, spots, size, size), F32)
    return pl.pallas_call(
        functools.partial(spread_kernel, grid, spots),
        out_shape=[shape, shape],
        in_specs=[pl.BlockSpec(memory_space=VMEM)] * 2,
        out_specs=[pl.BlockSpec(memory_space=VMEM)] * 2,
        scratch_shapes=[
            pltpu.SemaphoreType.DMA((2, grid)),
            pltpu.SemaphoreType.DMA((2, 2)),
            pltpu.SemaphoreType.DMA((2, 2, half)),
            pltpu.SemaphoreType.DMA((2, 2, half)),
        ],
        compiler_params=pltpu.CompilerParams(collective_id=3, has_side_effects=True),
        cost_estimate=pl.CostEstimate(flops=40_000_000, bytes_accessed=8 * rows.size, transcendentals=0),
        name="spread",
    )(rows, cols)


def split(value):
    high = value.astype(BF16)
    return high, (value - high.astype(F32)).astype(BF16)


def update_kernel(
    spots, row_ref, col_ref, where_ref, front_ref, r0, r1, rows_ref, cols_ref, low_ref, inv_ref, out_ref,
    v_rows, rows_high, rows_low, cols_high, cols_low,
):
    l = pl.program_id(0)
    size = front_ref.shape[-1]
    my_row, my_col = where_ref[1], where_ref[2]
    received = (r0, r1)

    @pl.when(l == 0)
    def _():
        for i in range(spots):
            here = pl.ds(i * size, size)
            v = mm_t(jnp.concatenate([rows_ref[0, i], rows_ref[1, i]], axis=1), inv_ref[...])
            if i == 0:
                low = jnp.where(my_row == 0, low_ref[0], low_ref[1])
                v = jnp.where(my_row < 2, low, v)
            v_rows[here, :] = v
            rows_high[here, :], rows_low[here, :] = split(v)
            w = mm_t(jnp.concatenate([cols_ref[0, i], cols_ref[1, i]], axis=1), inv_ref[...])
            cols_high[here, :], cols_low[here, :] = split(w)

    here = pl.ds(pl.multiple_of(l * size, size), size)
    high, low = rows_high[here, :], rows_low[here, :]
    top = (l == 0) & (my_row < 2)
    for j in range(spots):
        there = pl.ds(j * size, size)

        def dot(a, b):
            return lax.dot_general(a, b, (((1,), (1,)), ((), ())), preferred_element_type=F32)

        ch, cl = cols_high[there, :], cols_low[there, :]
        product = dot(high, ch) + (dot(high, cl) + dot(low, ch))
        parts = []
        for k in range(2):
            index = col_ref[k * spots + j]
            valid = (index >= 0) & (row_ref[k * spots + l] >= 0)
            parts.append((lambda i, k=k: received[k][i // 2, 0, 0, i % 2], index, valid))
        value = added(front_ref[pl.ds(j, size, stride=spots), :], parts) - product
        value = jnp.where(top, 0.0, value)
        if j == 0:
            v = v_rows[here, :]
            value = jnp.where(my_col == 0, v[:, :size], jnp.where(my_col == 1, v[:, size:], value))
        out_ref[pl.ds(j, size, stride=spots), :] = value


def update(flat, received, rows, cols, low, inverse, row_pos, col_pos, where):
    grid, _, blocks, _, size, _ = received.shape
    spots = rows.shape[1]

    def by_row(k):
        return pl.BlockSpec(
            (grid, 1, 1, 2, size, size),
            lambda l, row, *_: (0, k, jnp.maximum(row[k * spots + l], 0), 0, 0, 0),
        )

    def whole(value):
        zeros = (0,) * value.ndim
        return pl.BlockSpec(value.shape, lambda *_: zeros, pipeline_mode=pl.Buffered(1))

    line = pl.BlockSpec((size * spots, size), lambda l, *_: (l, 0))
    order = spots * size
    return pl.pallas_call(
        functools.partial(update_kernel, spots),
        grid_spec=pltpu.PrefetchScalarGridSpec(
            num_scalar_prefetch=3,
            grid=(spots,),
            in_specs=[line, by_row(0), by_row(1), whole(rows), whole(cols), whole(low), whole(inverse)],
            out_specs=line,
            scratch_shapes=[pltpu.VMEM((order, 2 * size), F32)] + [pltpu.VMEM((order, 2 * size), BF16)] * 4,
        ),
        out_shape=jax.ShapeDtypeStruct(flat.shape, F32),
        compiler_params=pltpu.CompilerParams(dimension_semantics=("arbitrary",)),
        cost_estimate=pl.CostEstimate(flops=4_000_000_000, bytes_accessed=12 * flat.size, transcendentals=0),
        name="update",
    )(row_pos.reshape(-1), col_pos.reshape(-1), where, flat, received, received, rows, cols, low, inverse)


def per_device(grid, orig_front, child_updates, index_maps):
    front, row, col = (lax.axis_index(name) for name in ("front", "row", "col"))
    local = orig_front[0, :, 0, :, :, 0, :]
    spots, size, _, _ = local.shape
    flat = local.reshape(spots * size * spots, size)
    child = child_updates[0, :, :, 0, :, :, 0, :]
    row_send, lead_row, lead_col, row_slot, col_send, row_pos, col_pos = tables(
        index_maps, front, row, col, grid, spots
    )
    where = jnp.stack([front, row, col]).astype(I32)
    fcol = local[:, :, 0, :]
    packed, lead = pack_rows(child, fcol[0], row_send, lead_row, lead_col, where, grid)
    lead = lax.psum(lead, ("front", "row", "col"))
    arrived = row_exchange(packed, grid)
    packed = pack_cols(arrived, row_slot, col_send, grid)
    lead = lax.dynamic_index_in_dim(lead, front, 0, keepdims=False)
    received, low, inverse = col_exchange(packed, lead, grid)
    rows, cols = panels(received, fcol, flat, row_pos, col_pos)
    rows, cols = spread(rows, cols, grid)
    out = update(flat, received, rows, cols, low, inverse, row_pos, col_pos, where)
    return out.reshape(1, spots, 1, size, spots, 1, size)


def solution(mesh):
    placed = (
        P("front", None, "row", None, None, "col", None),
        P("front", None, None, "row", None, None, "col", None),
        P(),
    )
    return jax.shard_map(
        functools.partial(per_device, mesh.shape["row"]),
        mesh=mesh,
        in_specs=placed,
        out_specs=P("front", None, "row", None, None, "col", None),
        check_vma=False,
    )
```

time: 918 us -> 475 us (0.52)
  waiting for transfers between devices: 485 us -> 124 us
  Pallas kernels: 0 us -> 316 us
  blocking collectives: 146 us -> 0 us
  matrix products: 84.9 us -> 0 us
  other arithmetic: 76.7 us -> 1.75 us
  local copies, waits for them, and re-layouts: 90.9 us -> 19.2 us
  starting transfers between devices: 12.5 us -> 0.01 us
    all_gather x6 -> x0, waiting for transfers between devices: 368 us -> none  [the longest x4 194 us: gather_axes(): value = lax.all_gather(value, axis, axis=dim, tiled=True)]
    pallas_call x0 -> x7, Pallas kernels: none -> 316 us  [the longest x1 99.9 us: col_exchange(): pl.pallas_call(functools.partial(col_exchange_kernel, grid, size), out_sh...]
    all_to_all x1 -> x0, blocking collectives: 146 us -> none  [per_device(): lax.all_to_all(by_cols, 'col', split_axis=0, concat_axis=0, tiled=True)]
    psum x0 -> x1, waiting for transfers between devices: none -> 124 us  [per_device(): lead = lax.psum(lead, ('front', 'row', 'col'))]
    all_to_all x2 -> x0, waiting for transfers between devices: 117 us -> none  [the longest x1 115 us: per_device(): lax.all_to_all(by_rows, ROW, split_axis=0, concat_axis=0, tiled=True)]
    dot_general x6 -> x0, matrix products: 65.9 us -> none  [the longest x1 20.1 us: per_device(): jnp.einsum('kcbm,ckixby->ixmy', col_place, col_incoming, preferred_elemen...]
    another operation x10 -> x1, other arithmetic: 45.7 us -> 0.67 us  [per_device(): where = jnp.stack([front, row, col]).astype(I32)]
    convert_element_type x2, local copies, waits for them, and re-layouts: 39.9 us -> 0.16 us  [the longest x1 0.08 us: tables(): row_hit = flat(own_target == row).astype(I32)]
  transfers between devices with their start and end apart: 8 -> 1, of which waited for: 8 -> 1; matrix products, arithmetic and copies ran while one was open for 0% -> 1% of each run, Pallas kernels for 0% -> 23%
where the time goes in v1:
time: 475 us; the launch traced here: 474 us
  Pallas kernels  316 us (67%)
  waiting for transfers between devices  124 us (26%)
  local copies, waits for them, and re-layouts  19.2 us (4%)
  between operations  13.6 us (3%)
    psum x1, waiting for transfers between devices, per_device(): lead = lax.psum(lead, ('front', 'row', 'col'))  124 us
    pallas_call x1, Pallas kernels, col_exchange(): pl.pallas_call(functools.partial(col_exchange_kernel, grid, size), out_sh...  99.9 us
    pallas_call x1, Pallas kernels, row_exchange(): pl.pallas_call(functools.partial(row_exchange_kernel, grid), out_shape=ja...  98.7 us
    pallas_call x1, Pallas kernels, spread(): pl.pallas_call(functools.partial(spread_kernel, grid, spots), out_shape=[...  64.5 us
    pallas_call x1, Pallas kernels, update(): pl.pallas_call(functools.partial(update_kernel, spots), grid_spec=pltpu.P...  25.2 us
    pallas_call x1, Pallas kernels, pack_rows(): pl.pallas_call(pack_rows_kernel, grid_spec=pltpu.PrefetchScalarGridSpec(n...  12 us
    pallas_call x1, Pallas kernels, pack_cols(): pl.pallas_call(pack_cols_kernel, grid_spec=pltpu.PrefetchScalarGridSpec(n...  11.5 us
  transfers between devices with their start and end apart: 1, of which 1 were waited for; matrix products, arithmetic and copies ran while one was open for 1% of the time, Pallas kernels for 23%

profile of v1, /device:TPU:4, one launch (start us, length us, event | category | flops | bytes accessed | tf_op | source)
XLA Modules:
  0.0 474.1 jit_solution(2670269211869040631)
XLA Ops:
  6.5 0.0 all-reduce.2.cloned.1.call-start
  6.6 0.8 reshape.166
  7.4 0.1 convert_reduce_fusion
  7.5 0.3 dynamic-slice_reduce_fusion
  7.8 0.1 fusion.5
  7.9 0.7 sub.34.lcol_ref
  8.6 0.6 reshape.170.slot_ref
  9.2 0.6 sub.32.lrow_ref
  9.8 5.0 %copy.47 = f32[1,12,1,128,12,1,128]{6,3,1,4,5,2,0:T(8,128)S(1)} copy(f32[1,12,1,128,12,1,128]{6,5,4,3,2,1,0:T(1,128)} %param.3) | data formatting | bytes 18874368 | tf_op args[0]
  14.8 0.0 copy-start
  14.8 3.7 copy-done
  18.5 0.6 slice_bitcast_fusion.1.corner_ref
  19.1 0.7 pad_add_fusion.where_ref
  19.8 12.0 %pack_rows.1 = (bf16[2,16,8,128,128]{4,3,2,1,0:T(8,128)(2,1)}, f32[2,2,2,128,128]{4,3,2,1,0:T(8,128)}) custom-call(s32[16]{0:T(128)} %reshape.170.slot_ref, s32[4]{0:T(128)} %sub.32.lrow_ref, s32[4]{0:T(128)} %sub.34.lcol_ref, s32[3]{0:T(128)} %pad_add_fusion.where_ref, bf16[2,8,128,8,128]{4,3,2,1,0:T(8,128)(2,1)} %bitcast.27, ...), custom_call_target="tpu_custom_call" | custom-call | flops 2000000 | bytes 8388608 | tf_op jit(solution)/shard_map/pack_rows/pallas_call | solution.py:89
  31.8 0.0 all-reduce.2.cloned.1.call-update
  31.9 0.2 dynamic-slice_reduce_fusion.3
  32.1 0.1 reshape.172
  32.2 0.1 reshape.167
  32.3 0.1 multiply_reduce_fusion
  32.4 0.1 multiply_reduce_fusion.3
  32.5 0.7 reshape.169.slot_ref
  33.2 0.1 eq.97
  33.3 0.7 reshape.168.row_ref
  33.9 0.1 reshape.173
  34.0 0.5 multiply_reduce_fusion.1
  34.5 0.1 copy.45
  34.6 0.6 sub.30.col_ref
  35.2 0.1 copy.44
  35.3 0.6 sub.28.row_ref
  35.9 98.7 %row_exchange.1.in_ref = bf16[2,16,8,128,128]{4,3,2,1,0:T(8,128)(2,1)} custom-call(bf16[2,16,8,128,128]{4,3,2,1,0:T(8,128)(2,1)} %get-tuple-element.14.send_ref), custom_call_target="tpu_custom_call" | custom-call | flops 100000000 | bytes 16777216 | tf_op jit(solution)/shard_map/row_exchange/pallas_call | solution.py:180
  134.6 11.5 %pack_cols.1.send_ref = bf16[2,8,16,128,128]{4,3,2,1,0:T(8,128)(2,1)} custom-call(s32[16]{0:T(128)} %reshape.168.row_ref, s32[16]{0:T(128)} %reshape.169.slot_ref, bf16[2,16,8,128,128]{4,3,2,1,0:T(8,128)(2,1)} %row_exchange.1.in_ref), custom_call_target="tpu_custom_call" | custom-call | flops 2000000 | bytes 16777216 | tf_op jit(solution)/shard_map/pack_cols/pallas_call | solution.py:123
  146.1 2.1 slice_bitcast_fusion.fcol_ref
  148.2 123.9 %all-reduce.2.cloned.1.call-done = f32[2,2,2,128,128]{4,3,2,1,0:T(8,128)} async-done(((f32[2,2,2,128,128]{4,3,2,1,0:T(8,128)}), f32[2,2,2,128,128]{4,3,2,1,0:T(8,128)}) %all-reduce.2.cloned.1.call-update) | async-done | bytes 524304 | tf_op jit(solution)/shard_map/psum | solution.py:578
  272.1 1.7 dynamic-slice_bitcast_fusion.lead_ref
  273.8 99.9 %col_exchange.1 = (bf16[8,2,8,2,128,128]{5,4,3,2,1,0:T(8,128)(2,1)}, f32[2,128,256]{2,1,0:T(8,128)}, f32[256,256]{1,0:T(8,128)}) custom-call(bf16[2,8,16,128,128]{4,3,2,1,0:T(8,128)(2,1)} %pack_cols.1.send_ref, f32[2,2,128,128]{3,2,1,0:T(8,128)} %dynamic-slice_bitcast_fusion.lead_ref), custom_call_target="tpu_custom_call" | custom-call | flops 100000000 | bytes 16777216 | tf_op jit(solution)/shard_map/col_exchange/pallas_call | solution.py:280
  373.7 4.0 panels.1
  377.6 64.5 %spread.1 = (f32[2,12,128,128]{3,2,1,0:T(8,128)}, f32[2,12,128,128]{3,2,1,0:T(8,128)}) custom-call(f32[12,128,128]{2,1,0:T(8,128)} %get-tuple-element.17.rows_ref, f32[12,128,128]{2,1,0:T(8,128)} %get-tuple-element.18.cols_ref), custom_call_target="tpu_custom_call" | custom-call | flops 40000000 | bytes 1572864 | tf_op jit(solution)/shard_map/spread/pallas_call | solution.py:466
  442.1 25.2 %update.1 = f32[18432,128]{1,0:T(8,128)} custom-call(s32[24]{0:T(128)} %sub.28.row_ref, s32[24]{0:T(128)} %sub.30.col_ref, s32[3]{0:T(128)} %pad_add_fusion.where_ref, f32[18432,128]{1,0:T(8,128)} %bitcast.24, bf16[8,2,8,2,128,128]{5,4,3,2,1,0:T(8,128)(2,1)} %get-tuple-element.16.c0.c1.r0.r1, bf16[8,2,8,2,128,128]{5,4,3,2,1,0:T(8,128)(2,1)} %get-tuple-element.16.c0.c1.r0.r1, ...), custom_call_target="tpu_custom_call" | custom-call | flops 4000000000 | bytes 28311552 | tf_op jit(solution)/shard_map/update/pallas_call | solution.py:550
  (15 shorter events, 0.1 us)
Async XLA Ops:
  6.5 265.5 %all-reduce.2.cloned.1.call-start = ((), (), s32[]{:S(2)}) async-start(), calls=%async_computation | async-start | bytes 1048576 | tf_op jit(solution)/shard_map/psum | solution.py:578
  14.8 3.7 copy-start
Sparse Core Ops, SparseCore 0:
  31.9 240.0 all-reduce.1

commit v2 on v1

--- a/solution.py
+++ b/solution.py
@@ -57,84 +57,9 @@
     at = (flat(own_place)[:, None, :] == spots[None, :, None]).astype(I32)
     row_pos = jnp.sum(row_hit[:, None, :] * at * (rank + 1)[:, None, :], axis=-1) - 1
     col_pos = jnp.sum(col_hit[:, None, :] * at * (flat(own_recv) + 1)[:, None, :], axis=-1) - 1
-    return row_send, lead_row, lead_col, row_slot, col_send, row_pos, col_pos
-
-
-def pack_rows_kernel(slot_ref, lrow_ref, lcol_ref, where_ref, child_ref, corner_ref, out_ref, lead_ref, wide):
-    p, q = pl.program_id(0), pl.program_id(1)
-    size, blocks = child_ref.shape[2], child_ref.shape[3]
-    wide[...] = child_ref[0, 0].astype(F32).reshape(size * blocks, size)
-
-    @pl.when(q == 0)
-    def _():
-        for a in range(2):
-            for b in range(2):
-                hit = (where_ref[0] == p) & (where_ref[1] == a) & (where_ref[2] == b)
-                lead_ref[0, a, b] = jnp.where(hit, corner_ref[...], 0.0)
-
-    for j in range(blocks):
-        out_ref[0, 0, j] = wide[pl.ds(j, size, stride=blocks), :].astype(BF16)
-
-    for a in range(2):
-        for b in range(2):
-
-            @pl.when((lrow_ref[2 * p + a] == q) & (lcol_ref[2 * p + b] >= 0))
-            def _():
-                j = jnp.maximum(lcol_ref[2 * p + b], 0)
-                lead_ref[0, a, b] = lead_ref[0, a, b] + out_ref[0, 0, j].astype(F32)
-
-
-def pack_rows(child, corner, slots, lead_row, lead_col, where, grid):
-    _, blocks, size, _, _ = child.shape
-    return pl.pallas_call(
-        pack_rows_kernel,
-        grid_spec=pltpu.PrefetchScalarGridSpec(
-            num_scalar_prefetch=4,
-            grid=(2, blocks),
-            in_specs=[
-                pl.BlockSpec((1, 1, size, blocks, size), lambda p, q, *_: (p, q, 0, 0, 0)),
-                pl.BlockSpec((size, size), lambda p, q, *_: (0, 0)),
-            ],
-            out_specs=[
-                pl.BlockSpec((1, 1, blocks, size, size), lambda p, q, s, *_: (p, s[p * blocks + q], 0, 0, 0)),
-                pl.BlockSpec((1, 2, 2, size, size), lambda p, q, *_: (p, 0, 0, 0, 0)),
-            ],
-            scratch_shapes=[pltpu.VMEM((size * blocks, size), F32)],
-        ),
-        out_shape=[
-            jax.ShapeDtypeStruct((2, grid * 2, blocks, size, size), BF16),
-            jax.ShapeDtypeStruct((2, 2, 2, size, size), F32),
-        ],
-        compiler_params=pltpu.CompilerParams(dimension_semantics=("arbitrary", "arbitrary")),
-        cost_estimate=pl.CostEstimate(flops=2_000_000, bytes_accessed=4 * child.size, transcendentals=0),
-        name="pack_rows",
-    )(slots.reshape(-1), lead_row.reshape(-1), lead_col.reshape(-1), where, child, corner)
-
-
-def pack_cols_kernel(row_ref, slot_ref, in_ref, out_ref):
-    k = pl.program_id(0)
-    blocks = in_ref.shape[2]
-    for j in range(blocks):
-        out_ref[0, 0, slot_ref[k * blocks + j]] = in_ref[0, 0, j]
-
-
-def pack_cols(received, row_slot, col_send, grid):
-    _, _, blocks, size, _ = received.shape
-    return pl.pallas_call(
-        pack_cols_kernel,
-        grid_spec=pltpu.PrefetchScalarGridSpec(
-            num_scalar_prefetch=2,
-            grid=(2, blocks),
-            in_specs=[
-                pl.BlockSpec((1, 1, blocks, size, size), lambda k, j, r, *_: (k, r[k * blocks + j], 0, 0, 0))
-            ],
-            out_specs=pl.BlockSpec((1, 1, grid * 2, size, size), lambda k, j, *_: (k, j, 0, 0, 0)),
-        ),
-        out_shape=jax.ShapeDtypeStruct((2, blocks, grid * 2, size, size), BF16),
-        compiler_params=pltpu.CompilerParams(dimension_semantics=("arbitrary", "arbitrary")),
-        cost_estimate=pl.CostEstimate(flops=2_000_000, bytes_accessed=4 * received.size, transcendentals=0),
-        name="pack_cols",
-    )(row_slot.reshape(-1), col_send.reshape(-1), received)
+    slots = jnp.arange(2 * grid, dtype=I32)
+    inverse = lambda sent: jnp.sum((sent[:, None, :] == slots[None, :, None]).astype(I32) * ids, axis=-1)
+    return inverse(row_send), lead_row, lead_col, row_slot, inverse(col_send), row_pos, col_pos
 
 
 def meet(peers):
@@ -146,51 +71,6 @@
 
 def hop_order(grid):
     return [d for pair in zip(range(1, grid), range(grid - 1, 0, -1)) for d in pair][: grid - 1]
-
-
-def row_exchange_kernel(grid, send_ref, recv_ref, send_sem, recv_sem, local_sem):
-    f, r, c = lax.axis_index("front"), lax.axis_index("row"), lax.axis_index("col")
-    others = [(p, d) for d in hop_order(grid) for p in range(2)] + [(1, 0)]
-    peers = [(lax.rem(f + p, 2), lax.rem(r + d, grid), c) for p, d in others]
-    local = pltpu.make_async_copy(send_ref.at[f, pl.ds(2 * r, 2)], recv_ref.at[f, pl.ds(2 * r, 2)], local_sem)
-    local.start()
-    meet(peers)
-    copies = []
-    for n, (p, d) in enumerate(others):
-        peer = peers[n]
-        copy = pltpu.make_async_remote_copy(
-            src_ref=send_ref.at[peer[0], pl.ds(2 * peer[1], 2)],
-            dst_ref=recv_ref.at[f, pl.ds(2 * r, 2)],
-            send_sem=send_sem.at[n],
-            recv_sem=recv_sem.at[p, d],
-            device_id=peer,
-            device_id_type=MESH,
-        )
-        copy.start()
-        copies.append(copy)
-    local.wait()
-    for copy in copies:
-        copy.wait_send()
-    for copy in copies:
-        copy.wait_recv()
-
-
-def row_exchange(packed, grid):
-    n = 2 * grid
-    return pl.pallas_call(
-        functools.partial(row_exchange_kernel, grid),
-        out_shape=jax.ShapeDtypeStruct(packed.shape, BF16),
-        in_specs=[pl.BlockSpec(memory_space=HBM)],
-        out_specs=pl.BlockSpec(memory_space=HBM),
-        scratch_shapes=[
-            pltpu.SemaphoreType.DMA((n,)),
-            pltpu.SemaphoreType.DMA((2, grid)),
-            pltpu.SemaphoreType.DMA,
-        ],
-        compiler_params=pltpu.CompilerParams(collective_id=1, has_side_effects=True),
-        cost_estimate=pl.CostEstimate(flops=100_000_000, bytes_accessed=4 * packed.size, transcendentals=0),
-        name="row_exchange",
-    )(packed)
 
 
 def factor_block(work, size):
@@ -231,12 +111,12 @@
     eye = (
         lax.broadcasted_iota(I32, (size, size), 0) == lax.broadcasted_iota(I32, (size, size), 1)
     ).astype(F32)
-    work[:, :size] = lead_ref[0, 0]
+    work[:, :size] = lead_ref[:size]
     work[:, size:] = eye
     factor_block(work, size)
     l0, i0 = triangular(work, size)
-    l10 = mm_t(lead_ref[1, 0], i0)
-    work[:, :size] = lead_ref[1, 1] - mm_t(l10, l10)
+    l10 = mm_t(lead_ref[size : 2 * size], i0)
+    work[:, :size] = lead_ref[2 * size :] - mm_t(l10, l10)
     work[:, size:] = eye
     factor_block(work, size)
     l1, i1 = triangular(work, size)
@@ -248,58 +128,233 @@
     inv_ref[size:, size:] = i1
 
 
-def col_exchange_kernel(grid, size, send_ref, lead_ref, recv_ref, low_ref, inv_ref, work, send_sem, recv_sem, local_sem):
+LEAD = ((0, 0), (1, 0), (1, 1))
+
+
+def exchange_kernel(
+    grid, size, blocks, spots,
+    rows_inv, row_slot, cols_inv, lead_row, lead_col, child_hbm, flat_hbm,
+    recv_two, low_ref, inv_ref, fcol_ref,
+    child, send_one, recv_one, turned, send_two, wide, chunk, part, sum_one, sum_two, got_one, got_two, lead, work,
+    child_sem, chunk_sem, local_sem, one_send, one_recv, two_send, two_recv,
+    la_send, la_recv, lb_send, lb_recv, lc_send, lc_recv,
+):
     f, r, c = lax.axis_index("front"), lax.axis_index("row"), lax.axis_index("col")
-    others = hop_order(grid)
-    peers = [(f, r, lax.rem(c + d, grid)) for d in others]
-    local = pltpu.make_async_copy(send_ref.at[:, :, pl.ds(2 * c, 2)], recv_ref.at[c], local_sem)
-    local.start()
-    meet(peers)
-    copies = []
-    for n, d in enumerate(others):
-        copy = pltpu.make_async_remote_copy(
-            src_ref=send_ref.at[:, :, pl.ds(2 * peers[n][2], 2)],
-            dst_ref=recv_ref.at[c],
-            send_sem=send_sem.at[n],
-            recv_sem=recv_sem.at[d],
-            device_id=peers[n],
-            device_id_type=MESH,
+    other = 1 - f
+    piece = len(LEAD) * size // grid
+    steps = hop_order(grid)
+    row_peers = [(0, d) for d in steps] + [(1, 0)] + [(1, d) for d in steps]
+    row_at = lambda p, d: (lax.rem(f + p, 2), lax.rem(r + d, grid), c)
+    col_at = lambda d: (f, r, lax.rem(c + d, grid))
+
+    def remote(src, dst, send_sem, recv_sem, peer):
+        return pltpu.make_async_remote_copy(
+            src_ref=src, dst_ref=dst, send_sem=send_sem, recv_sem=recv_sem, device_id=peer, device_id_type=MESH
+        )
+
+    def line(n, slot):
+        rows = pl.ds(n * size * spots, size * spots)
+        return pltpu.make_async_copy(flat_hbm.at[rows], chunk.at[slot], chunk_sem.at[slot])
+
+    loads = [pltpu.make_async_copy(child_hbm.at[p], child.at[p], child_sem.at[p]) for p in range(2)]
+    for load in loads:
+        load.start()
+    line(0, 0).start()
+    meet([row_at(p, d) for p, d in row_peers] + [col_at(d) for d in steps])
+    for load in loads:
+        load.wait()
+    line(0, 0).wait()
+
+    corner = chunk[0, pl.ds(0, size, stride=spots), :]
+    lane = lax.broadcasted_iota(I32, (size, blocks, size), 1)
+    for p in range(2):
+        for n, (a, b) in enumerate(LEAD):
+            qa, qb = lead_row[2 * p + a], lead_col[2 * p + b]
+            block = child[p, jnp.maximum(qa, 0)].astype(F32)
+            block = jnp.sum(jnp.where(lane == qb, block, 0.0), axis=1)
+            block = jnp.where((qa >= 0) & (qb >= 0), block, 0.0)
+            mine = (f == p) & (r == a) & (c == b)
+            part[p, pl.ds(n * size, size)] = block + jnp.where(mine, corner, 0.0)
+    round_a = []
+    for n, (p, d) in enumerate(row_peers):
+        peer = row_at(p, d)
+        copy = remote(
+            part.at[peer[0], pl.ds(peer[1] * piece, piece)],
+            got_one.at[f, r], la_send.at[n], la_recv.at[p, d], peer,
         )
         copy.start()
-        copies.append(copy)
-    factor_lead(lead_ref, low_ref, inv_ref, work, size)
-    local.wait()
-    for copy in copies:
+        round_a.append(copy)
+
+    round_one = []
+    for p in range(2):
+        for n, (q, d) in enumerate(row_peers):
+            if q != p:
+                continue
+            peer = row_at(p, d)
+            for s in range(2):
+                slot = 2 * peer[1] + s
+                send_one[peer[0], slot] = child[peer[0], rows_inv[peer[0] * 2 * grid + slot]]
+            copy = remote(
+                send_one.at[peer[0], pl.ds(2 * peer[1], 2)],
+                recv_one.at[f, pl.ds(2 * r, 2)], one_send.at[n], one_recv.at[p, d], peer,
+            )
+            copy.start()
+            round_one.append(copy)
+
+    def turn(source, k, slot):
+        wide[...] = source.astype(F32).reshape(size * blocks, size)
+        for j in range(blocks):
+            turned[k, slot, j] = wide[pl.ds(j, size, stride=blocks), :].astype(BF16)
+
+    def turn_own(s, carry):
+        slot = 2 * r + s
+        turn(child[f, rows_inv[f * 2 * grid + slot]], f, slot)
+        return carry
+
+    lax.fori_loop(0, 2, turn_own, 0)
+
+    for copy in round_a:
+        copy.wait_recv()
+    got_one[f, r] = part[f, pl.ds(pl.multiple_of(r * piece, 8), piece)]
+    total = got_one[0, 0]
+    for k in range(2):
+        for n in range(grid):
+            if k + n > 0:
+                total = total + got_one[k, n]
+    sum_one[...] = total
+    got_two[c] = total
+    round_b = []
+    for n, d in enumerate(steps):
+        copy = remote(sum_one, got_two.at[c], lb_send.at[n], lb_recv.at[d], col_at(d))
+        copy.start()
+        round_b.append(copy)
+
+    def finish_child(p):
+        k = f if p == 0 else other
+        for n, (q, d) in enumerate(row_peers):
+            if q != p:
+                continue
+            round_one[n].wait_recv()
+            source = lax.rem(r + grid - d, grid)
+
+            def turn_one(s, carry):
+                turn(recv_one[k, 2 * source + s], k, 2 * source + s)
+                return carry
+
+            lax.fori_loop(0, 2, turn_one, 0)
+
+        def gather(j, carry):
+            row = row_slot[k * blocks + j]
+            for slot in range(2 * grid):
+                send_two[k, slot // 2, j, slot % 2] = turned[k, row, cols_inv[k * 2 * grid + slot]]
+            return carry
+
+        lax.fori_loop(0, blocks, gather, 0)
+        sent = []
+        for n, d in enumerate(steps):
+            peer = col_at(d)
+            copy = remote(
+                send_two.at[k, peer[2]], recv_two.at[c, k], two_send.at[p, n], two_recv.at[k, d], peer
+            )
+            copy.start()
+            sent.append(copy)
+        local = pltpu.make_async_copy(send_two.at[k, c], recv_two.at[c, k], local_sem.at[p])
+        local.start()
+        return sent, local
+
+    sent_a, local_a = finish_child(0)
+
+    for copy in round_b:
+        copy.wait_recv()
+    total = got_two[0]
+    for n in range(1, grid):
+        total = total + got_two[n]
+    sum_two[...] = total
+    lead[pl.ds(pl.multiple_of(r * piece, 8), piece)] = total
+    round_c = []
+    for n, d in enumerate(steps):
+        copy = remote(
+            sum_two, lead.at[pl.ds(pl.multiple_of(r * piece, 8), piece)], lc_send.at[n], lc_recv.at[d], row_at(0, d)
+        )
+        copy.start()
+        round_c.append(copy)
+
+    sent_b, local_b = finish_child(1)
+
+    for n in range(spots):
+        line(n, n % 2).start()
+        if n > 0:
+            line(n - 1, (n - 1) % 2).wait()
+            fcol_ref[n - 1] = chunk[(n - 1) % 2, pl.ds(0, size, stride=spots), :]
+    line(spots - 1, (spots - 1) % 2).wait()
+    fcol_ref[spots - 1] = chunk[(spots - 1) % 2, pl.ds(0, size, stride=spots), :]
+
+    for n, d in enumerate(steps):
+        source = pl.ds(pl.multiple_of(lax.rem(r + grid - d, grid) * piece, 8), piece)
+        remote(sum_two, lead.at[source], lc_send.at[n], lc_recv.at[d], row_at(0, d)).wait_recv()
+    factor_lead(lead, low_ref, inv_ref, work, size)
+
+    for copy in round_a + round_b + round_c + round_one:
         copy.wait_send()
-    for copy in copies:
-        copy.wait_recv()
-
-
-def col_exchange(packed, lead, grid):
-    _, blocks, _, size, _ = packed.shape
+    for sent, local, k in ((sent_a, local_a, f), (sent_b, local_b, other)):
+        local.wait()
+        for n, d in enumerate(steps):
+            sent[n].wait_send()
+            sent[n].wait_recv()
+
+
+def exchange(child, flat, rows_inv, row_slot, cols_inv, lead_row, lead_col, grid, spots):
+    _, blocks, size, _, _ = child.shape
+    piece = len(LEAD) * size // grid
+    dma = pltpu.SemaphoreType.DMA
+    smem = pl.BlockSpec(memory_space=SMEM)
+    hbm = pl.BlockSpec(memory_space=HBM)
+    vmem = pl.BlockSpec(memory_space=VMEM)
     return pl.pallas_call(
-        functools.partial(col_exchange_kernel, grid, size),
+        functools.partial(exchange_kernel, grid, size, blocks, spots),
         out_shape=[
             jax.ShapeDtypeStruct((grid, 2, blocks, 2, size, size), BF16),
             jax.ShapeDtypeStruct((2, size, 2 * size), F32),
             jax.ShapeDtypeStruct((2 * size, 2 * size), F32),
+            jax.ShapeDtypeStruct((spots, size, size), F32),
         ],
-        in_specs=[pl.BlockSpec(memory_space=HBM), pl.BlockSpec(memory_space=VMEM)],
-        out_specs=[
-            pl.BlockSpec(memory_space=HBM),
-            pl.BlockSpec(memory_space=VMEM),
-            pl.BlockSpec(memory_space=VMEM),
+        in_specs=[smem] * 5 + [hbm] * 2,
+        out_specs=[hbm, vmem, vmem, vmem],
+        scratch_shapes=[
+            pltpu.VMEM(child.shape, BF16),
+            pltpu.VMEM((2, 2 * grid, size, blocks, size), BF16),
+            pltpu.VMEM((2, 2 * grid, size, blocks, size), BF16),
+            pltpu.VMEM((2, 2 * grid, blocks, size, size), BF16),
+            pltpu.VMEM((2, grid, blocks, 2, size, size), BF16),
+            pltpu.VMEM((size * blocks, size), F32),
+            pltpu.VMEM((2, size * spots, size), F32),
+            pltpu.VMEM((2, len(LEAD) * size, size), F32),
+            pltpu.VMEM((piece, size), F32),
+            pltpu.VMEM((piece, size), F32),
+            pltpu.VMEM((2, grid, piece, size), F32),
+            pltpu.VMEM((grid, piece, size), F32),
+            pltpu.VMEM((len(LEAD) * size, size), F32),
+            pltpu.VMEM((size, 2 * size), F32),
+            dma((2,)),
+            dma((2,)),
+            dma((2,)),
+            dma((2 * grid,)),
+            dma((2, grid)),
+            dma((2, grid)),
+            dma((2, grid)),
+            dma((2 * grid,)),
+            dma((2, grid)),
+            dma((grid,)),
+            dma((grid,)),
+            dma((grid,)),
+            dma((grid,)),
         ],
-        scratch_shapes=[
-            pltpu.VMEM((size, 2 * size), F32),
-            pltpu.SemaphoreType.DMA((grid,)),
-            pltpu.SemaphoreType.DMA((grid,)),
-            pltpu.SemaphoreType.DMA,
-        ],
-        compiler_params=pltpu.CompilerParams(collective_id=2, has_side_effects=True),
-        cost_estimate=pl.CostEstimate(flops=100_000_000, bytes_accessed=4 * packed.size, transcendentals=0),
-        name="col_exchange",
-    )(packed, lead)
+        compiler_params=pltpu.CompilerParams(
+            collective_id=1, has_side_effects=True, vmem_limit_bytes=60 * 2**20
+        ),
+        cost_estimate=pl.CostEstimate(flops=400_000_000, bytes_accessed=8 * child.size, transcendentals=0),
+        name="exchange",
+    )(rows_inv.reshape(-1), row_slot.reshape(-1), cols_inv.reshape(-1), lead_row.reshape(-1), lead_col.reshape(-1), child, flat)
 
 
 def added(base, parts):
@@ -569,17 +624,13 @@
     spots, size, _, _ = local.shape
     flat = local.reshape(spots * size * spots, size)
     child = child_updates[0, :, :, 0, :, :, 0, :]
-    row_send, lead_row, lead_col, row_slot, col_send, row_pos, col_pos = tables(
+    rows_inv, lead_row, lead_col, row_slot, cols_inv, row_pos, col_pos = tables(
         index_maps, front, row, col, grid, spots
     )
     where = jnp.stack([front, row, col]).astype(I32)
-    fcol = local[:, :, 0, :]
-    packed, lead = pack_rows(child, fcol[0], row_send, lead_row, lead_col, where, grid)
-    lead = lax.psum(lead, ("front", "row", "col"))
-    arrived = row_exchange(packed, grid)
-    packed = pack_cols(arrived, row_slot, col_send, grid)
-    lead = lax.dynamic_index_in_dim(lead, front, 0, keepdims=False)
-    received, low, inverse = col_exchange(packed, lead, grid)
+    received, low, inverse, fcol = exchange(
+        child, flat, rows_inv, row_slot, cols_inv, lead_row, lead_col, grid, spots
+    )
     rows, cols = panels(received, fcol, flat, row_pos, col_pos)
     rows, cols = spread(rows, cols, grid)
     out = update(flat, received, rows, cols, low, inverse, row_pos, col_pos, where)

time: 475 us -> 315 us (0.66)
  waiting for transfers between devices: 124 us -> 0 us
  between operations: 13.6 us -> 0.1 us
  local copies, waits for them, and re-layouts: 19.2 us -> 6.17 us
  Pallas kernels: 316 us -> 307 us
    psum x1 -> x0, waiting for transfers between devices: 124 us -> none  [per_device(): lead = lax.psum(lead, ('front', 'row', 'col'))]
    unnamed x5 -> x2, local copies, waits for them, and re-layouts: 8.91 us -> 0.18 us
    pallas_call x4 -> x1, Pallas kernels: 222 us -> 216 us  [exchange(): pl.pallas_call(functools.partial(exchange_kernel, grid, size, blocks, spo...]
  transfers between devices with their start and end apart: 1 -> 0, of which waited for: 1 -> 0; matrix products, arithmetic and copies ran while one was open for 1% -> 0% of each run, Pallas kernels for 23% -> 0%
where the time goes in v2:
time: 315 us
  Pallas kernels  307 us (97%)
  local copies, waits for them, and re-layouts  6.17 us (2%)
    pallas_call x1, Pallas kernels, exchange(): pl.pallas_call(functools.partial(exchange_kernel, grid, size, blocks, spo...  216 us
    pallas_call x1, Pallas kernels, spread(): pl.pallas_call(functools.partial(spread_kernel, grid, spots), out_shape=[...  61.4 us
    pallas_call x1, Pallas kernels, update(): pl.pallas_call(functools.partial(update_kernel, spots), grid_spec=pltpu.P...  24.9 us

profile of v2, /device:TPU:4, one launch (start us, length us, event | category | flops | bytes accessed | tf_op | source)
XLA Modules:
  0.0 314.8 jit_solution(2678626767351976299)
XLA Ops:
  0.0 0.7 pad_add_fusion.where_ref
  0.7 0.8 reshape.166
  1.5 0.1 convert_reduce_fusion
  1.7 0.3 dynamic-slice_reduce_fusion
  1.9 0.2 dynamic-slice_reduce_fusion.2
  2.2 0.1 reshape.172
  2.2 0.1 multiply_reduce_fusion
  2.3 0.1 select_reduce_fusion
  2.4 0.6 reshape.170.cols_inv
  3.1 0.1 fusion.5
  3.2 0.6 sub.34.lead_col
  3.8 0.1 eq.127
  3.9 0.1 reshape.167
  4.0 0.1 multiply_reduce_fusion.3
  4.1 0.6 reshape.169.row_slot
  4.8 0.7 sub.32.lead_row
  5.4 0.1 select_reduce_fusion.1
  5.5 0.6 reshape.168.rows_inv
  6.1 0.1 reshape.173
  6.2 0.5 multiply_reduce_fusion.1
  6.7 0.1 copy.40
  6.8 0.7 sub.30.col_ref
  7.4 0.1 copy.39
  7.5 0.7 sub.28.row_ref
  8.2 216.3 %exchange.1 = (bf16[8,2,8,2,128,128]{5,4,3,2,1,0:T(8,128)(2,1)}, f32[2,128,256]{2,1,0:T(8,128)}, f32[256,256]{1,0:T(8,128)}, f32[12,128,128]{2,1,0:T(8,128)}) custom-call(s32[32]{0:T(128)} %reshape.168.rows_inv, s32[16]{0:T(128)} %reshape.169.row_slot, s32[32]{0:T(128)} %reshape.170.cols_inv, s32[4]{0:T(128)} %sub.32.lead_row, s32[4]{0:T(128)} %sub.34.lead_col, ...), custom_call_target="tpu_custom_call" | custom-call | flops 400000000 | bytes 16777216 | tf_op jit(solution)/shard_map/exchange/pallas_call | solution.py:313
  224.5 4.0 %panels.1 = (f32[12,128,128]{2,1,0:T(8,128)}, f32[12,128,128]{2,1,0:T(8,128)}) custom-call(s32[24]{0:T(128)} %sub.28.row_ref, s32[24]{0:T(128)} %sub.30.col_ref, f32[12,128,128]{2,1,0:T(8,128)} %get-tuple-element.14.fcol_ref, f32[18432,128]{1,0:T(8,128)} %bitcast.15, bf16[8,2,8,2,128,128]{5,4,3,2,1,0:T(8,128)(2,1)} %get-tuple-element.13.c0.c1.r0.r1, ...), custom_call_target="tpu_custom_call" | custom-call | flops 2000000 | bytes 6000000 | tf_op jit(solution)/shard_map/panels/pallas_call | solution.py:404
  228.4 61.4 %spread.1 = (f32[2,12,128,128]{3,2,1,0:T(8,128)}, f32[2,12,128,128]{3,2,1,0:T(8,128)}) custom-call(f32[12,128,128]{2,1,0:T(8,128)} %get-tuple-element.15.rows_ref, f32[12,128,128]{2,1,0:T(8,128)} %get-tuple-element.16.cols_ref), custom_call_target="tpu_custom_call" | custom-call | flops 40000000 | bytes 1572864 | tf_op jit(solution)/shard_map/spread/pallas_call | solution.py:521
  289.9 24.9 %update.1 = f32[18432,128]{1,0:T(8,128)} custom-call(s32[24]{0:T(128)} %sub.28.row_ref, s32[24]{0:T(128)} %sub.30.col_ref, s32[3]{0:T(128)} %pad_add_fusion.where_ref, f32[18432,128]{1,0:T(8,128)} %bitcast.16, bf16[8,2,8,2,128,128]{5,4,3,2,1,0:T(8,128)(2,1)} %get-tuple-element.13.c0.c1.r0.r1, bf16[8,2,8,2,128,128]{5,4,3,2,1,0:T(8,128)(2,1)} %get-tuple-element.13.c0.c1.r0.r1, ...), custom_call_target="tpu_custom_call" | custom-call | flops 4000000000 | bytes 28311552 | tf_op jit(solution)/shard_map/update/pallas_call | solution.py:605
  (15 shorter events, 0.1 us)

commit v3 on v2

--- a/solution.py
+++ b/solution.py
@@ -250,19 +250,24 @@
             return carry
 
         lax.fori_loop(0, blocks, gather, 0)
-        sent = []
-        for n, d in enumerate(steps):
-            peer = col_at(d)
-            copy = remote(
-                send_two.at[k, peer[2]], recv_two.at[c, k], two_send.at[p, n], two_recv.at[k, d], peer
-            )
-            copy.start()
-            sent.append(copy)
         local = pltpu.make_async_copy(send_two.at[k, c], recv_two.at[c, k], local_sem.at[p])
         local.start()
-        return sent, local
-
-    sent_a, local_a = finish_child(0)
+        return local
+
+    def send_child(p, which):
+        k = f if p == 0 else other
+        for n, d in enumerate(steps):
+            if d % 2 == which:
+                peer = col_at(d)
+                copy = remote(
+                    send_two.at[k, peer[2]], recv_two.at[c, k], two_send.at[p, n], two_recv.at[k, d], peer
+                )
+                copy.start()
+                round_two.append(copy)
+
+    round_two = []
+    local_a = finish_child(0)
+    send_child(0, 0)
 
     for copy in round_b:
         copy.wait_recv()
@@ -279,7 +284,10 @@
         copy.start()
         round_c.append(copy)
 
-    sent_b, local_b = finish_child(1)
+    local_b = finish_child(1)
+    send_child(0, 1)
+    send_child(1, 1)
+    send_child(1, 0)
 
     for n in range(spots):
         line(n, n % 2).start()
@@ -296,11 +304,11 @@
 
     for copy in round_a + round_b + round_c + round_one:
         copy.wait_send()
-    for sent, local, k in ((sent_a, local_a, f), (sent_b, local_b, other)):
-        local.wait()
-        for n, d in enumerate(steps):
-            sent[n].wait_send()
-            sent[n].wait_recv()
+    local_a.wait()
+    local_b.wait()
+    for copy in round_two:
+        copy.wait_send()
+        copy.wait_recv()
 
 
 def exchange(child, flat, rows_inv, row_slot, cols_inv, lead_row, lead_col, grid, spots):

time: 315 us -> 321 us (1.019); the launches traced: 315 us -> 317 us
    pallas_call x1, Pallas kernels: 61.4 us -> 67.1 us  [spread(): pl.pallas_call(functools.partial(spread_kernel, grid, spots), out_shape=[...]
    pallas_call x1, Pallas kernels: 216 us -> 212 us  [exchange(): pl.pallas_call(functools.partial(exchange_kernel, grid, size, blocks, spo...]
where the time goes in v3:
time: 321 us; the launch traced here: 317 us
  Pallas kernels  308 us (96%)
  local copies, waits for them, and re-layouts  6.17 us (2%)
    pallas_call x1, Pallas kernels, exchange(): pl.pallas_call(functools.partial(exchange_kernel, grid, size, blocks, spo...  212 us
    pallas_call x1, Pallas kernels, spread(): pl.pallas_call(functools.partial(spread_kernel, grid, spots), out_shape=[...  67.1 us
    pallas_call x1, Pallas kernels, update(): pl.pallas_call(functools.partial(update_kernel, spots), grid_spec=pltpu.P...  25.1 us

profile of v3, /device:TPU:4, one launch (start us, length us, event | category | flops | bytes accessed | tf_op | source)
XLA Modules:
  0.0 316.5 jit_solution(9850701272999376725)
XLA Ops:
  0.0 0.7 pad_add_fusion.where_ref
  0.7 0.8 reshape.166
  1.5 0.1 convert_reduce_fusion
  1.7 0.3 dynamic-slice_reduce_fusion
  1.9 0.2 dynamic-slice_reduce_fusion.2
  2.2 0.1 reshape.172
  2.2 0.1 multiply_reduce_fusion
  2.3 0.1 select_reduce_fusion
  2.4 0.6 reshape.170.cols_inv
  3.1 0.1 fusion.5
  3.2 0.6 sub.34.lead_col
  3.8 0.1 eq.127
  3.9 0.1 reshape.167
  4.0 0.1 multiply_reduce_fusion.3
  4.1 0.6 reshape.169.row_slot
  4.8 0.7 sub.32.lead_row
  5.4 0.1 select_reduce_fusion.1
  5.5 0.6 reshape.168.rows_inv
  6.1 0.1 reshape.173
  6.2 0.5 multiply_reduce_fusion.1
  6.7 0.1 copy.40
  6.8 0.7 sub.30.col_ref
  7.4 0.1 copy.39
  7.5 0.7 sub.28.row_ref
  8.2 212.2 %exchange.1 = (bf16[8,2,8,2,128,128]{5,4,3,2,1,0:T(8,128)(2,1)}, f32[2,128,256]{2,1,0:T(8,128)}, f32[256,256]{1,0:T(8,128)}, f32[12,128,128]{2,1,0:T(8,128)}) custom-call(s32[32]{0:T(128)} %reshape.168.rows_inv, s32[16]{0:T(128)} %reshape.169.row_slot, s32[32]{0:T(128)} %reshape.170.cols_inv, s32[4]{0:T(128)} %sub.32.lead_row, s32[4]{0:T(128)} %sub.34.lead_col, ...), custom_call_target="tpu_custom_call" | custom-call | flops 400000000 | bytes 16777216 | tf_op jit(solution)/shard_map/exchange/pallas_call | solution.py:321
  220.4 4.0 %panels.1 = (f32[12,128,128]{2,1,0:T(8,128)}, f32[12,128,128]{2,1,0:T(8,128)}) custom-call(s32[24]{0:T(128)} %sub.28.row_ref, s32[24]{0:T(128)} %sub.30.col_ref, f32[12,128,128]{2,1,0:T(8,128)} %get-tuple-element.14.fcol_ref, f32[18432,128]{1,0:T(8,128)} %bitcast.15, bf16[8,2,8,2,128,128]{5,4,3,2,1,0:T(8,128)(2,1)} %get-tuple-element.13.c0.c1.r0.r1, ...), custom_call_target="tpu_custom_call" | custom-call | flops 2000000 | bytes 6000000 | tf_op jit(solution)/shard_map/panels/pallas_call | solution.py:412
  224.3 67.1 %spread.1 = (f32[2,12,128,128]{3,2,1,0:T(8,128)}, f32[2,12,128,128]{3,2,1,0:T(8,128)}) custom-call(f32[12,128,128]{2,1,0:T(8,128)} %get-tuple-element.15.rows_ref, f32[12,128,128]{2,1,0:T(8,128)} %get-tuple-element.16.cols_ref), custom_call_target="tpu_custom_call" | custom-call | flops 40000000 | bytes 1572864 | tf_op jit(solution)/shard_map/spread/pallas_call | solution.py:529
  291.4 25.1 %update.1 = f32[18432,128]{1,0:T(8,128)} custom-call(s32[24]{0:T(128)} %sub.28.row_ref, s32[24]{0:T(128)} %sub.30.col_ref, s32[3]{0:T(128)} %pad_add_fusion.where_ref, f32[18432,128]{1,0:T(8,128)} %bitcast.16, bf16[8,2,8,2,128,128]{5,4,3,2,1,0:T(8,128)(2,1)} %get-tuple-element.13.c0.c1.r0.r1, bf16[8,2,8,2,128,128]{5,4,3,2,1,0:T(8,128)(2,1)} %get-tuple-element.13.c0.c1.r0.r1, ...), custom_call_target="tpu_custom_call" | custom-call | flops 4000000000 | bytes 28311552 | tf_op jit(solution)/shard_map/update/pallas_call | solution.py:613
  (15 shorter events, 0.1 us)

commit v4 on v2

--- a/solution.py
+++ b/solution.py
@@ -73,6 +73,16 @@
     return [d for pair in zip(range(1, grid), range(grid - 1, 0, -1)) for d in pair][: grid - 1]
 
 
+def codes(half, flip_cost):
+    pairs = [(n, flip) for n in range(half) for flip in range(2) if n + flip > 0]
+    return sorted(pairs, key=lambda pair: -(min(pair[0], half - pair[0]) + flip_cost * pair[1]))
+
+
+def member(me, code, half, sign=1):
+    ring = lax.rem(me // 2 + (half + sign * code[0]), half)
+    return 2 * ring + lax.rem(me + code[1], 2)
+
+
 def factor_block(work, size):
     lanes = lax.broadcasted_iota(I32, (size, size), 1)
     rows = lax.broadcasted_iota(I32, (size, 1), 0)
@@ -142,10 +152,12 @@
     f, r, c = lax.axis_index("front"), lax.axis_index("row"), lax.axis_index("col")
     other = 1 - f
     piece = len(LEAD) * size // grid
-    steps = hop_order(grid)
-    row_peers = [(0, d) for d in steps] + [(1, 0)] + [(1, d) for d in steps]
-    row_at = lambda p, d: (lax.rem(f + p, 2), lax.rem(r + d, grid), c)
-    col_at = lambda d: (f, r, lax.rem(c + d, grid))
+    half = grid // 2
+    row_steps, col_steps = codes(half, 1), codes(half, 2)
+    row_peers = [(0, d) for d in row_steps] + [(1, d) for d in row_steps] + [(1, (0, 0))]
+    row_at = lambda p, d: (lax.rem(f + p, 2), member(r, d, half), c)
+    col_at = lambda d: (f, r, member(c, d, half))
+    code_of = lambda d: 2 * d[0] + d[1]
 
     def remote(src, dst, send_sem, recv_sem, peer):
         return pltpu.make_async_remote_copy(
@@ -160,7 +172,7 @@
     for load in loads:
         load.start()
     line(0, 0).start()
-    meet([row_at(p, d) for p, d in row_peers] + [col_at(d) for d in steps])
+    meet([row_at(p, d) for p, d in row_peers] + [col_at(d) for d in col_steps])
     for load in loads:
         load.wait()
     line(0, 0).wait()
@@ -180,7 +192,7 @@
         peer = row_at(p, d)
         copy = remote(
             part.at[peer[0], pl.ds(peer[1] * piece, piece)],
-            got_one.at[f, r], la_send.at[n], la_recv.at[p, d], peer,
+            got_one.at[f, r], la_send.at[n], la_recv.at[p, code_of(d)], peer,
         )
         copy.start()
         round_a.append(copy)
@@ -196,7 +208,7 @@
                 send_one[peer[0], slot] = child[peer[0], rows_inv[peer[0] * 2 * grid + slot]]
             copy = remote(
                 send_one.at[peer[0], pl.ds(2 * peer[1], 2)],
-                recv_one.at[f, pl.ds(2 * r, 2)], one_send.at[n], one_recv.at[p, d], peer,
+                recv_one.at[f, pl.ds(2 * r, 2)], one_send.at[n], one_recv.at[p, code_of(d)], peer,
             )
             copy.start()
             round_one.append(copy)
@@ -224,8 +236,8 @@
     sum_one[...] = total
     got_two[c] = total
     round_b = []
-    for n, d in enumerate(steps):
-        copy = remote(sum_one, got_two.at[c], lb_send.at[n], lb_recv.at[d], col_at(d))
+    for n, d in enumerate(col_steps):
+        copy = remote(sum_one, got_two.at[c], lb_send.at[n], lb_recv.at[code_of(d)], col_at(d))
         copy.start()
         round_b.append(copy)
 
@@ -235,7 +247,7 @@
             if q != p:
                 continue
             round_one[n].wait_recv()
-            source = lax.rem(r + grid - d, grid)
+            source = member(r, d, half, -1)
 
             def turn_one(s, carry):
                 turn(recv_one[k, 2 * source + s], k, 2 * source + s)
@@ -251,10 +263,10 @@
 
         lax.fori_loop(0, blocks, gather, 0)
         sent = []
-        for n, d in enumerate(steps):
+        for n, d in enumerate(col_steps):
             peer = col_at(d)
             copy = remote(
-                send_two.at[k, peer[2]], recv_two.at[c, k], two_send.at[p, n], two_recv.at[k, d], peer
+                send_two.at[k, peer[2]], recv_two.at[c, k], two_send.at[p, n], two_recv.at[k, code_of(d)], peer
             )
             copy.start()
             sent.append(copy)
@@ -272,9 +284,9 @@
     sum_two[...] = total
     lead[pl.ds(pl.multiple_of(r * piece, 8), piece)] = total
     round_c = []
-    for n, d in enumerate(steps):
+    for n, d in enumerate(row_steps):
         copy = remote(
-            sum_two, lead.at[pl.ds(pl.multiple_of(r * piece, 8), piece)], lc_send.at[n], lc_recv.at[d], row_at(0, d)
+            sum_two, lead.at[pl.ds(pl.multiple_of(r * piece, 8), piece)], lc_send.at[n], lc_recv.at[code_of(d)], row_at(0, d)
         )
         copy.start()
         round_c.append(copy)
@@ -289,16 +301,16 @@
     line(spots - 1, (spots - 1) % 2).wait()
     fcol_ref[spots - 1] = chunk[(spots - 1) % 2, pl.ds(0, size, stride=spots), :]
 
-    for n, d in enumerate(steps):
-        source = pl.ds(pl.multiple_of(lax.rem(r + grid - d, grid) * piece, 8), piece)
-        remote(sum_two, lead.at[source], lc_send.at[n], lc_recv.at[d], row_at(0, d)).wait_recv()
+    for n, d in enumerate(row_steps):
+        source = pl.ds(pl.multiple_of(member(r, d, half, -1) * piece, 8), piece)
+        remote(sum_two, lead.at[source], lc_send.at[n], lc_recv.at[code_of(d)], row_at(0, d)).wait_recv()
     factor_lead(lead, low_ref, inv_ref, work, size)
 
     for copy in round_a + round_b + round_c + round_one:
         copy.wait_send()
     for sent, local, k in ((sent_a, local_a, f), (sent_b, local_b, other)):
         local.wait()
-        for n, d in enumerate(steps):
+        for n in range(len(sent)):
             sent[n].wait_send()
             sent[n].wait_recv()
 

time: 315 us -> 311 us (0.987)
  Pallas kernels: 307 us -> 301 us
    pallas_call x1, Pallas kernels: 61.4 us -> 54.7 us  [spread(): pl.pallas_call(functools.partial(spread_kernel, grid, spots), out_shape=[...]
where the time goes in v4:
time: 311 us; the launch traced here: 309 us
  Pallas kernels  301 us (97%)
  local copies, waits for them, and re-layouts  6.17 us (2%)
    pallas_call x1, Pallas kernels, exchange(): pl.pallas_call(functools.partial(exchange_kernel, grid, size, blocks, spo...  217 us
    pallas_call x1, Pallas kernels, spread(): pl.pallas_call(functools.partial(spread_kernel, grid, spots), out_shape=[...  54.7 us
    pallas_call x1, Pallas kernels, update(): pl.pallas_call(functools.partial(update_kernel, spots), grid_spec=pltpu.P...  25.2 us

profile of v4, /device:TPU:4, one launch (start us, length us, event | category | flops | bytes accessed | tf_op | source)
XLA Modules:
  0.0 309.1 jit_solution(1241713419505075735)
XLA Ops:
  0.0 0.7 pad_add_fusion.where_ref
  0.7 0.8 reshape.166
  1.5 0.1 convert_reduce_fusion
  1.7 0.3 dynamic-slice_reduce_fusion
  1.9 0.2 dynamic-slice_reduce_fusion.2
  2.2 0.1 reshape.172
  2.2 0.1 multiply_reduce_fusion
  2.3 0.1 select_reduce_fusion
  2.4 0.6 reshape.170.cols_inv
  3.1 0.1 fusion.5
  3.2 0.6 sub.34.lead_col
  3.8 0.1 eq.127
  3.9 0.1 reshape.167
  4.0 0.1 multiply_reduce_fusion.3
  4.1 0.6 reshape.169.row_slot
  4.8 0.7 sub.32.lead_row
  5.4 0.1 select_reduce_fusion.1
  5.5 0.6 reshape.168.rows_inv
  6.1 0.1 reshape.173
  6.2 0.5 multiply_reduce_fusion.1
  6.7 0.1 copy.40
  6.8 0.7 sub.30.col_ref
  7.4 0.1 copy.39
  7.5 0.7 sub.28.row_ref
  8.2 217.1 %exchange.1 = (bf16[8,2,8,2,128,128]{5,4,3,2,1,0:T(8,128)(2,1)}, f32[2,128,256]{2,1,0:T(8,128)}, f32[256,256]{1,0:T(8,128)}, f32[12,128,128]{2,1,0:T(8,128)}) custom-call(s32[32]{0:T(128)} %reshape.168.rows_inv, s32[16]{0:T(128)} %reshape.169.row_slot, s32[32]{0:T(128)} %reshape.170.cols_inv, s32[4]{0:T(128)} %sub.32.lead_row, s32[4]{0:T(128)} %sub.34.lead_col, ...), custom_call_target="tpu_custom_call" | custom-call | flops 400000000 | bytes 16777216 | tf_op jit(solution)/shard_map/exchange/pallas_call | solution.py:325
  225.3 4.0 %panels.1 = (f32[12,128,128]{2,1,0:T(8,128)}, f32[12,128,128]{2,1,0:T(8,128)}) custom-call(s32[24]{0:T(128)} %sub.28.row_ref, s32[24]{0:T(128)} %sub.30.col_ref, f32[12,128,128]{2,1,0:T(8,128)} %get-tuple-element.14.fcol_ref, f32[18432,128]{1,0:T(8,128)} %bitcast.15, bf16[8,2,8,2,128,128]{5,4,3,2,1,0:T(8,128)(2,1)} %get-tuple-element.13.c0.c1.r0.r1, ...), custom_call_target="tpu_custom_call" | custom-call | flops 2000000 | bytes 6000000 | tf_op jit(solution)/shard_map/panels/pallas_call | solution.py:416
  229.2 54.7 %spread.1 = (f32[2,12,128,128]{3,2,1,0:T(8,128)}, f32[2,12,128,128]{3,2,1,0:T(8,128)}) custom-call(f32[12,128,128]{2,1,0:T(8,128)} %get-tuple-element.15.rows_ref, f32[12,128,128]{2,1,0:T(8,128)} %get-tuple-element.16.cols_ref), custom_call_target="tpu_custom_call" | custom-call | flops 40000000 | bytes 1572864 | tf_op jit(solution)/shard_map/spread/pallas_call | solution.py:533
  283.9 25.2 %update.1 = f32[18432,128]{1,0:T(8,128)} custom-call(s32[24]{0:T(128)} %sub.28.row_ref, s32[24]{0:T(128)} %sub.30.col_ref, s32[3]{0:T(128)} %pad_add_fusion.where_ref, f32[18432,128]{1,0:T(8,128)} %bitcast.16, bf16[8,2,8,2,128,128]{5,4,3,2,1,0:T(8,128)(2,1)} %get-tuple-element.13.c0.c1.r0.r1, bf16[8,2,8,2,128,128]{5,4,3,2,1,0:T(8,128)(2,1)} %get-tuple-element.13.c0.c1.r0.r1, ...), custom_call_target="tpu_custom_call" | custom-call | flops 4000000000 | bytes 28311552 | tf_op jit(solution)/shard_map/update/pallas_call | solution.py:617
  (15 shorter events, 0.1 us)

commit v5 on v4

--- a/solution.py
+++ b/solution.py
@@ -370,78 +370,71 @@
 
 
 def added(base, parts):
-    for ref, index, valid in parts:
-        base = base + jnp.where(valid, ref(jnp.maximum(index, 0)).astype(F32), 0.0)
+    for block, valid in parts:
+        base = base + jnp.where(valid, block.astype(F32), 0.0)
     return base
 
 
-def panel_kernel(spots, row_ref, col_ref, fcol_ref, frow_ref, c0, c1, r0, r1, rows_out, cols_out):
-    size = fcol_ref.shape[-1]
-    cols = (c0, c1)
-    rows = (r0, r1)
-    for l in range(spots):
-        parts = []
-        for k in range(2):
-            index = row_ref[k * spots + l]
-            valid = (index >= 0) & (col_ref[k * spots] >= 0)
-            parts.append((lambda i, k=k: cols[k][0, 0, i, 0], index, valid))
-        rows_out[l] = added(fcol_ref[l], parts)
-        parts = []
-        for k in range(2):
-            index = col_ref[k * spots + l]
-            valid = (index >= 0) & (row_ref[k * spots] >= 0)
-            parts.append((lambda i, k=k: rows[k][i // 2, 0, 0, i % 2], index, valid))
-        cols_out[l] = added(frow_ref[pl.ds(l, size, stride=spots), :], parts).T
-
-
-def panels(received, fcol, flat, row_pos, col_pos):
-    grid, _, blocks, _, size, _ = received.shape
-    spots = fcol.shape[0]
-
-    def by_col(k):
-        def index(_, row, col):
-            i = jnp.maximum(col[k * spots], 0)
-            return (i // 2, k, 0, i % 2, 0, 0)
-
-        return pl.BlockSpec((1, 1, blocks, 1, size, size), index)
-
-    def by_row(k):
-        return pl.BlockSpec(
-            (grid, 1, 1, 2, size, size),
-            lambda _, row, col: (0, k, jnp.maximum(row[k * spots], 0), 0, 0, 0),
-        )
-
-    shape = jax.ShapeDtypeStruct((spots, size, size), F32)
-    whole = pl.BlockSpec((spots, size, size), lambda *_: (0, 0, 0))
-    return pl.pallas_call(
-        functools.partial(panel_kernel, spots),
-        grid_spec=pltpu.PrefetchScalarGridSpec(
-            num_scalar_prefetch=2,
-            grid=(1,),
-            in_specs=[
-                whole,
-                pl.BlockSpec((size * spots, size), lambda *_: (0, 0)),
-                by_col(0),
-                by_col(1),
-                by_row(0),
-                by_row(1),
-            ],
-            out_specs=[whole, whole],
-        ),
-        out_shape=[shape, shape],
-        cost_estimate=pl.CostEstimate(flops=2_000_000, bytes_accessed=6_000_000, transcendentals=0),
-        name="panels",
-    )(row_pos.reshape(-1), col_pos.reshape(-1), fcol, flat, received, received, received, received)
-
-
-def spread_kernel(grid, spots, rows_ref, cols_ref, rows_out, cols_out, one_send, one_recv, two_send, two_recv):
+def split(value):
+    high = value.astype(BF16)
+    return high, (value - high.astype(F32)).astype(BF16)
+
+
+def spread_kernel(
+    grid, spots, size, row_ref, col_ref, child_hbm, flat_hbm, fcol_ref, low_ref, inv_ref,
+    whole_hbm, v_rows, rows_high, rows_low, cols_high, cols_low,
+    child, whole, rows_own, cols_own, rows_all, cols_all,
+    child_sem, in_sem, out_sem, one_send, one_recv, two_send, two_recv,
+):
     f, r, c = lax.axis_index("front"), lax.axis_index("row"), lax.axis_index("col")
     half = grid // 2
     part = spots // half
     row_peer = lambda i: (f, r, i)
     col_peer = lambda i: (f, i, c)
-    groups = ((rows_ref, rows_out, c, row_peer), (cols_ref, cols_out, r, col_peer))
+    groups = ((rows_own, rows_all, c, row_peer), (cols_own, cols_all, r, col_peer))
+    order = hop_order(grid)
+
+    def line(l):
+        return pl.ds(pl.multiple_of(l * size * spots, size * spots), size * spots)
+
+    def line_in(l):
+        return pltpu.make_async_copy(flat_hbm.at[line(l)], whole.at[line(l)], in_sem.at[l])
+
+    def line_out(l):
+        return pltpu.make_async_copy(whole.at[line(l)], whole_hbm.at[line(l)], out_sem.at[l])
+
+    line_in(0).start()
+    for n in range(grid):
+        pltpu.make_async_copy(child_hbm.at[n], child.at[n], child_sem.at[n]).start()
+    for l in range(1, spots):
+        line_in(l).start()
     meet([peer(lax.rem(me + d, grid)) for _, _, me, peer in groups for d in range(1, grid)])
+
+    def from_child(l, j):
+        parts = []
+        for k in range(2):
+            row, col = row_ref[k * spots + l], col_ref[k * spots + j]
+            valid = (row >= 0) & (col >= 0)
+            row, col = jnp.maximum(row, 0), jnp.maximum(col, 0)
+            parts.append((child[col // 2, k, row, col % 2], valid))
+        return parts
+
+    line_in(0).wait()
+    for n in range(grid):
+        pltpu.make_async_copy(child_hbm.at[n], child.at[n], child_sem.at[n]).wait()
+
+    @pl.when(c < 2)
+    def _():
+        def one(l, carry):
+            rows_own[l] = added(fcol_ref[l], from_child(l, 0))
+            return carry
+
+        lax.fori_loop(0, spots, one, 0)
+
+    @pl.when(r < 2)
+    def _():
+        for j in range(spots):
+            cols_own[j] = added(whole[pl.ds(j, size, stride=spots), :], from_child(0, j)).T
 
     def first(g, s, n):
         source, out, me, peer = groups[g]
@@ -473,7 +466,7 @@
 
             @pl.when(groups[g][2] == s)
             def _():
-                for n in hop_order(grid):
+                for n in order:
                     first(g, s, n).start()
 
     for g in range(2):
@@ -485,6 +478,19 @@
                 out[s, pl.ds(0, part)] = source[pl.ds(0, part)]
                 for n in range(1, half):
                     second(g, s, n, source).start()
+
+    def assemble(l, carry):
+        @pl.when(l > 0)
+        def _():
+            line_in(l).wait()
+
+        for j in range(spots):
+            here = pl.ds(l * size * spots + j, size, stride=spots)
+            whole[here, :] = added(whole[here, :], from_child(l, j))
+        line_out(l).start()
+        return carry
+
+    lax.fori_loop(0, spots, assemble, 0)
 
     for g in range(2):
         _, out, me, _ = groups[g]
@@ -504,18 +510,33 @@
                 for n in range(1, half):
                     second(g, s, n, out.at[s]).start()
 
+    def solve(g, quarter):
+        out = groups[g][1]
+
+        def one(i, carry):
+            l = quarter * part + i
+            here = pl.ds(pl.multiple_of(l * size, size), size)
+            v = mm_t(jnp.concatenate([out[0, l], out[1, l]], axis=1), inv_ref[...])
+            if g == 0:
+                low = jnp.where(r == 0, low_ref[0], low_ref[1])
+                v = jnp.where((r < 2) & (l == 0), low, v)
+                v_rows[here, :] = v
+                rows_high[here, :], rows_low[here, :] = split(v)
+            else:
+                cols_high[here, :], cols_low[here, :] = split(v)
+            return carry
+
+        lax.fori_loop(0, part, one, 0)
+
     for g in range(2):
-        source, out, me, _ = groups[g]
-        for s in range(2):
-
-            @pl.when(me == s)
-            def _():
-                for n in hop_order(grid):
-                    first(g, s, n).wait_send()
-
-            for n in range(1, half):
-                second(g, s, n, out.at[s]).wait_send()
-                piece = pl.ds(lax.rem(me // 2 + half - n, half) * part, part)
+        solve(g, groups[g][2] // 2)
+
+    for n in range(1, half):
+        for g in range(2):
+            source, out, me, _ = groups[g]
+            quarter = lax.rem(me // 2 + half - n, half)
+            piece = pl.ds(quarter * part, part)
+            for s in range(2):
                 pltpu.make_async_remote_copy(
                     src_ref=out.at[s, piece],
                     dst_ref=out.at[s, piece],
@@ -524,110 +545,105 @@
                     device_id=groups[g][3](lax.rem(me + 2 * n, grid)),
                     device_id_type=MESH,
                 ).wait_recv()
-
-
-def spread(rows, cols, grid):
-    spots, size, _ = rows.shape
+            solve(g, quarter)
+
+    for g in range(2):
+        _, out, me, _ = groups[g]
+        for s in range(2):
+
+            @pl.when(me == s)
+            def _():
+                for n in order:
+                    first(g, s, n).wait_send()
+
+            for n in range(1, half):
+                second(g, s, n, out.at[s]).wait_send()
+    for l in range(spots):
+        line_out(l).wait()
+
+
+def spread(received, flat, fcol, low, inverse, row_pos, col_pos, grid):
+    spots, size, _ = fcol.shape
     half = grid // 2
-    shape = jax.ShapeDtypeStruct((2, spots, size, size), F32)
+    order = spots * size
+    dma = pltpu.SemaphoreType.DMA
+    smem = pl.BlockSpec(memory_space=SMEM)
+    hbm = pl.BlockSpec(memory_space=HBM)
+    vmem = pl.BlockSpec(memory_space=VMEM)
     return pl.pallas_call(
-        functools.partial(spread_kernel, grid, spots),
-        out_shape=[shape, shape],
-        in_specs=[pl.BlockSpec(memory_space=VMEM)] * 2,
-        out_specs=[pl.BlockSpec(memory_space=VMEM)] * 2,
+        functools.partial(spread_kernel, grid, spots, size),
+        out_shape=[jax.ShapeDtypeStruct(flat.shape, F32), jax.ShapeDtypeStruct((order, 2 * size), F32)]
+        + [jax.ShapeDtypeStruct((order, 2 * size), BF16)] * 4,
+        in_specs=[smem] * 2 + [hbm] * 2 + [vmem] * 3,
+        out_specs=[hbm] + [vmem] * 5,
         scratch_shapes=[
-            pltpu.SemaphoreType.DMA((2, grid)),
-            pltpu.SemaphoreType.DMA((2, 2)),
-            pltpu.SemaphoreType.DMA((2, 2, half)),
-            pltpu.SemaphoreType.DMA((2, 2, half)),
+            pltpu.VMEM(received.shape, BF16),
+            pltpu.VMEM(flat.shape, F32),
+            pltpu.VMEM((spots, size, size), F32),
+            pltpu.VMEM((spots, size, size), F32),
+            pltpu.VMEM((2, spots, size, size), F32),
+            pltpu.VMEM((2, spots, size, size), F32),
+            dma((grid,)),
+            dma((spots,)),
+            dma((spots,)),
+            dma((2, grid)),
+            dma((2, 2)),
+            dma((2, 2, half)),
+            dma((2, 2, half)),
         ],
-        compiler_params=pltpu.CompilerParams(collective_id=3, has_side_effects=True),
-        cost_estimate=pl.CostEstimate(flops=40_000_000, bytes_accessed=8 * rows.size, transcendentals=0),
+        compiler_params=pltpu.CompilerParams(
+            collective_id=3, has_side_effects=True, vmem_limit_bytes=48 * 2**20
+        ),
+        cost_estimate=pl.CostEstimate(flops=40_000_000, bytes_accessed=8 * flat.size, transcendentals=0),
         name="spread",
-    )(rows, cols)
-
-
-def split(value):
-    high = value.astype(BF16)
-    return high, (value - high.astype(F32)).astype(BF16)
-
-
-def update_kernel(
-    spots, row_ref, col_ref, where_ref, front_ref, r0, r1, rows_ref, cols_ref, low_ref, inv_ref, out_ref,
-    v_rows, rows_high, rows_low, cols_high, cols_low,
-):
-    l = pl.program_id(0)
-    size = front_ref.shape[-1]
+    )(row_pos.reshape(-1), col_pos.reshape(-1), received, flat, fcol, low, inverse)
+
+
+def update_kernel(spots, size, where_ref, whole_ref, v_rows, rows_high, rows_low, cols_high, cols_low, out_ref):
+    step = pl.program_id(0)
     my_row, my_col = where_ref[1], where_ref[2]
-    received = (r0, r1)
-
-    @pl.when(l == 0)
-    def _():
-        for i in range(spots):
-            here = pl.ds(i * size, size)
-            v = mm_t(jnp.concatenate([rows_ref[0, i], rows_ref[1, i]], axis=1), inv_ref[...])
-            if i == 0:
-                low = jnp.where(my_row == 0, low_ref[0], low_ref[1])
-                v = jnp.where(my_row < 2, low, v)
-            v_rows[here, :] = v
-            rows_high[here, :], rows_low[here, :] = split(v)
-            w = mm_t(jnp.concatenate([cols_ref[0, i], cols_ref[1, i]], axis=1), inv_ref[...])
-            cols_high[here, :], cols_low[here, :] = split(w)
-
-    here = pl.ds(pl.multiple_of(l * size, size), size)
-    high, low = rows_high[here, :], rows_low[here, :]
-    top = (l == 0) & (my_row < 2)
-    for j in range(spots):
-        there = pl.ds(j * size, size)
-
-        def dot(a, b):
-            return lax.dot_general(a, b, (((1,), (1,)), ((), ())), preferred_element_type=F32)
-
+    count = whole_ref.shape[0] // (size * spots)
+    wide = 2 if spots % 2 == 0 else 1
+
+    def dot(a, b):
+        return lax.dot_general(a, b, (((1,), (1,)), ((), ())), preferred_element_type=F32)
+
+    high, low = rows_high[...], rows_low[...]
+    for j in range(0, spots, wide):
+        there = pl.ds(j * size, wide * size)
         ch, cl = cols_high[there, :], cols_low[there, :]
         product = dot(high, ch) + (dot(high, cl) + dot(low, ch))
-        parts = []
-        for k in range(2):
-            index = col_ref[k * spots + j]
-            valid = (index >= 0) & (row_ref[k * spots + l] >= 0)
-            parts.append((lambda i, k=k: received[k][i // 2, 0, 0, i % 2], index, valid))
-        value = added(front_ref[pl.ds(j, size, stride=spots), :], parts) - product
-        value = jnp.where(top, 0.0, value)
-        if j == 0:
-            v = v_rows[here, :]
-            value = jnp.where(my_col == 0, v[:, :size], jnp.where(my_col == 1, v[:, size:], value))
-        out_ref[pl.ds(j, size, stride=spots), :] = value
-
-
-def update(flat, received, rows, cols, low, inverse, row_pos, col_pos, where):
-    grid, _, blocks, _, size, _ = received.shape
-    spots = rows.shape[1]
-
-    def by_row(k):
-        return pl.BlockSpec(
-            (grid, 1, 1, 2, size, size),
-            lambda l, row, *_: (0, k, jnp.maximum(row[k * spots + l], 0), 0, 0, 0),
-        )
-
-    def whole(value):
-        zeros = (0,) * value.ndim
-        return pl.BlockSpec(value.shape, lambda *_: zeros, pipeline_mode=pl.Buffered(1))
-
-    line = pl.BlockSpec((size * spots, size), lambda l, *_: (l, 0))
-    order = spots * size
+        for i in range(count):
+            top = (step == 0) & (my_row < 2) & (i == 0)
+            for w in range(wide):
+                here = pl.ds(i * size * spots + j + w, size, stride=spots)
+                value = whole_ref[here, :] - product[i * size : (i + 1) * size, w * size : (w + 1) * size]
+                value = jnp.where(top, 0.0, value)
+                if j + w == 0:
+                    v = v_rows[pl.ds(i * size, size), :]
+                    value = jnp.where(my_col == 0, v[:, :size], jnp.where(my_col == 1, v[:, size:], value))
+                out_ref[here, :] = value
+
+
+def update(whole, v_rows, rows_high, rows_low, cols_high, cols_low, where, spots):
+    size = whole.shape[-1]
+    count = 2 if spots % 2 == 0 else 1
+    line = pl.BlockSpec((count * size * spots, size), lambda l, *_: (l, 0))
+    rows = pl.BlockSpec((count * size, 2 * size), lambda l, *_: (l, 0))
+    cols = pl.BlockSpec((spots * size, 2 * size), lambda l, *_: (0, 0), pipeline_mode=pl.Buffered(1))
     return pl.pallas_call(
-        functools.partial(update_kernel, spots),
+        functools.partial(update_kernel, spots, size),
         grid_spec=pltpu.PrefetchScalarGridSpec(
-            num_scalar_prefetch=3,
-            grid=(spots,),
-            in_specs=[line, by_row(0), by_row(1), whole(rows), whole(cols), whole(low), whole(inverse)],
+            num_scalar_prefetch=1,
+            grid=(spots // count,),
+            in_specs=[line, rows, rows, rows, cols, cols],
             out_specs=line,
-            scratch_shapes=[pltpu.VMEM((order, 2 * size), F32)] + [pltpu.VMEM((order, 2 * size), BF16)] * 4,
         ),
-        out_shape=jax.ShapeDtypeStruct(flat.shape, F32),
+        out_shape=jax.ShapeDtypeStruct(whole.shape, F32),
         compiler_params=pltpu.CompilerParams(dimension_semantics=("arbitrary",)),
-        cost_estimate=pl.CostEstimate(flops=4_000_000_000, bytes_accessed=12 * flat.size, transcendentals=0),
+        cost_estimate=pl.CostEstimate(flops=4_000_000_000, bytes_accessed=8 * whole.size, transcendentals=0),
         name="update",
-    )(row_pos.reshape(-1), col_pos.reshape(-1), where, flat, received, received, rows, cols, low, inverse)
+    )(where, whole, v_rows, rows_high, rows_low, cols_high, cols_low)
 
 
 def per_device(grid, orig_front, child_updates, index_maps):
@@ -643,9 +659,8 @@
     received, low, inverse, fcol = exchange(
         child, flat, rows_inv, row_slot, cols_inv, lead_row, lead_col, grid, spots
     )
-    rows, cols = panels(received, fcol, flat, row_pos, col_pos)
-    rows, cols = spread(rows, cols, grid)
-    out = update(flat, received, rows, cols, low, inverse, row_pos, col_pos, where)
+    whole, *factors = spread(received, flat, fcol, low, inverse, row_pos, col_pos, grid)
+    out = update(whole, *factors, where, spots)
     return out.reshape(1, spots, 1, size, spots, 1, size)
 
 

time: 311 us -> 303 us (0.974)
  Pallas kernels: 301 us -> 286 us
  local copies, waits for them, and re-layouts: 6.17 us -> 12.8 us
    pallas_call x3 -> x2, Pallas kernels: 83.9 us -> 69.2 us  [the longest x1 56.7 us: spread(): pl.pallas_call(functools.partial(spread_kernel, grid, spots, size), out_s...]
    unnamed x2 -> x18, local copies, waits for them, and re-layouts: 0.18 us -> 7.96 us
where the time goes in v5:
time: 303 us; the launch traced here: 301 us
  Pallas kernels  286 us (94%)
  local copies, waits for them, and re-layouts  12.8 us (4%)
    pallas_call x1, Pallas kernels, exchange(): pl.pallas_call(functools.partial(exchange_kernel, grid, size, blocks, spo...  217 us
    pallas_call x1, Pallas kernels, spread(): pl.pallas_call(functools.partial(spread_kernel, grid, spots, size), out_s...  56.7 us
    pallas_call x1, Pallas kernels, update(): pl.pallas_call(functools.partial(update_kernel, spots, size), grid_spec=p...  12.6 us
    unnamed x18, local copies, waits for them, and re-layouts  7.96 us

profile of v5, /device:TPU:4, one launch (start us, length us, event | category | flops | bytes accessed | tf_op | source)
XLA Modules:
  0.0 301.0 jit_solution(11333965823423751378)
XLA Ops:
  0.0 0.6 pad_add_fusion.where_ref
  0.6 0.8 reshape.164
  1.4 0.1 convert_reduce_fusion
  1.6 0.3 dynamic-slice_reduce_fusion
  1.8 0.2 dynamic-slice_reduce_fusion.2
  2.1 0.1 reshape.170
  2.2 0.1 multiply_reduce_fusion
  2.3 0.1 select_reduce_fusion
  2.4 0.6 reshape.168.cols_inv
  3.0 0.1 fusion.5
  3.1 0.6 sub.34.lead_col
  3.7 0.1 eq.127
  3.8 0.1 reshape.165
  3.9 0.1 multiply_reduce_fusion.3
  4.0 0.6 reshape.167.row_slot
  4.7 0.7 sub.32.lead_row
  5.3 0.1 select_reduce_fusion.1
  5.4 0.6 reshape.166.rows_inv
  6.0 0.1 reshape.171
  6.1 0.5 multiply_reduce_fusion.1
  6.6 0.1 copy.40
  6.7 0.1 sub.30.col_ref
  6.8 0.1 copy.39
  6.9 0.1 sub.28.row_ref
  7.0 217.0 %exchange.1 = (bf16[8,2,8,2,128,128]{5,4,3,2,1,0:T(8,128)(2,1)}, f32[2,128,256]{2,1,0:T(8,128)}, f32[256,256]{1,0:T(8,128)}, f32[12,128,128]{2,1,0:T(8,128)}) custom-call(s32[32]{0:T(128)} %reshape.166.rows_inv, s32[16]{0:T(128)} %reshape.167.row_slot, s32[32]{0:T(128)} %reshape.168.cols_inv, s32[4]{0:T(128)} %sub.32.lead_row, s32[4]{0:T(128)} %sub.34.lead_col, ...), custom_call_target="tpu_custom_call" | custom-call | flops 400000000 | bytes 16777216 | tf_op jit(solution)/shard_map/exchange/pallas_call | solution.py:325
  224.0 0.0 copy-start.1
  224.0 1.1 copy-done.1
  225.1 0.0 copy-start.6
  225.1 0.9 copy-done.6
  226.1 0.0 copy-start.7
  226.1 0.9 copy-done.7
  227.0 56.7 %spread.1 = (f32[18432,128]{1,0:T(8,128)}, f32[1536,256]{1,0:T(8,128)S(1)}, bf16[1536,256]{1,0:T(8,128)(2,1)S(1)}, bf16[1536,256]{1,0:T(8,128)(2,1)S(1)}, bf16[1...) custom-call(s32[24]{0:T(128)S(1)} %sub.28.row_ref, s32[24]{0:T(128)S(1)} %sub.30.col_ref, ...), custom_call_target="tpu_custom_call" | custom-call | flops 40000000 | bytes 18874368 | tf_op jit(solution)/shard_map/spread/pallas_call | solution.py:573
  283.7 0.0 copy-start
  283.7 1.2 copy-done
  284.9 0.0 copy-start.2
  284.9 0.9 copy-done.2
  285.8 0.0 copy-start.3
  285.8 0.9 copy-done.3
  286.7 0.0 copy-start.4
  286.7 0.9 copy-done.4
  287.6 0.0 copy-start.5
  287.6 0.9 copy-done.5
  288.5 12.6 %update.1 = f32[18432,128]{1,0:T(8,128)} custom-call(s32[3]{0:T(128)} %pad_add_fusion.where_ref, f32[18432,128]{1,0:T(8,128)} %get-tuple-element.19.whole_ref, f32[1536,256]{1,0:T(8,128)} %copy-done, bf16[1536,256]{1,0:T(8,128)(2,1)} %copy-done.2, bf16[1536,256]{1,0:T(8,128)(2,1)} %copy-done.3, bf16[1536,256]{1,0:T(8,128)(2,1)} %copy-done.4, ...), custom_call_target="tpu_custom_call" | custom-call | flops 4000000000 | bytes 18874368 | tf_op jit(solution)/shard_map/update/pallas_call | solution.py:634
  (15 shorter events, 0.1 us)
Async XLA Ops:
  224.0 1.1 copy-start.1
  225.1 0.9 copy-start.6
  226.1 0.9 copy-start.7
  283.7 1.2 copy-start
  284.9 0.9 copy-start.2
  285.8 0.9 copy-start.3
  286.7 0.9 copy-start.4
  287.6 0.9 copy-start.5

commit v6 on v5

--- a/solution.py
+++ b/solution.py
@@ -144,9 +144,9 @@
 def exchange_kernel(
     grid, size, blocks, spots,
     rows_inv, row_slot, cols_inv, lead_row, lead_col, child_hbm, flat_hbm,
-    recv_two, low_ref, inv_ref, fcol_ref,
-    child, send_one, recv_one, turned, send_two, wide, chunk, part, sum_one, sum_two, got_one, got_two, lead, work,
-    child_sem, chunk_sem, local_sem, one_send, one_recv, two_send, two_recv,
+    recv_two, low_out, inv_out, fcol_out,
+    low_ref, inv_ref, fcol_ref, child, send_one, recv_one, turned, send_two, wide, chunk, part, sum_one, sum_two, got_one, got_two, lead, work,
+    child_sem, chunk_sem, local_sem, out_sem, one_send, one_recv, two_send, two_recv,
     la_send, la_recv, lb_send, lb_recv, lc_send, lc_recv,
 ):
     f, r, c = lax.axis_index("front"), lax.axis_index("row"), lax.axis_index("col")
@@ -197,33 +197,13 @@
         copy.start()
         round_a.append(copy)
 
-    round_one = []
     for p in range(2):
-        for n, (q, d) in enumerate(row_peers):
-            if q != p:
-                continue
-            peer = row_at(p, d)
-            for s in range(2):
-                slot = 2 * peer[1] + s
-                send_one[peer[0], slot] = child[peer[0], rows_inv[peer[0] * 2 * grid + slot]]
-            copy = remote(
-                send_one.at[peer[0], pl.ds(2 * peer[1], 2)],
-                recv_one.at[f, pl.ds(2 * r, 2)], one_send.at[n], one_recv.at[p, code_of(d)], peer,
-            )
-            copy.start()
-            round_one.append(copy)
-
-    def turn(source, k, slot):
-        wide[...] = source.astype(F32).reshape(size * blocks, size)
-        for j in range(blocks):
-            turned[k, slot, j] = wide[pl.ds(j, size, stride=blocks), :].astype(BF16)
-
-    def turn_own(s, carry):
-        slot = 2 * r + s
-        turn(child[f, rows_inv[f * 2 * grid + slot]], f, slot)
-        return carry
-
-    lax.fori_loop(0, 2, turn_own, 0)
+        for q, d in row_peers:
+            if q == p:
+                front, row, _ = row_at(p, d)
+                for s in range(2):
+                    slot = 2 * row + s
+                    send_one[front, slot] = child[front, rows_inv[front * 2 * grid + slot]]
 
     for copy in round_a:
         copy.wait_recv()
@@ -241,40 +221,17 @@
         copy.start()
         round_b.append(copy)
 
-    def finish_child(p):
-        k = f if p == 0 else other
-        for n, (q, d) in enumerate(row_peers):
-            if q != p:
-                continue
-            round_one[n].wait_recv()
-            source = member(r, d, half, -1)
-
-            def turn_one(s, carry):
-                turn(recv_one[k, 2 * source + s], k, 2 * source + s)
-                return carry
-
-            lax.fori_loop(0, 2, turn_one, 0)
-
-        def gather(j, carry):
-            row = row_slot[k * blocks + j]
-            for slot in range(2 * grid):
-                send_two[k, slot // 2, j, slot % 2] = turned[k, row, cols_inv[k * 2 * grid + slot]]
-            return carry
-
-        lax.fori_loop(0, blocks, gather, 0)
-        sent = []
-        for n, d in enumerate(col_steps):
-            peer = col_at(d)
-            copy = remote(
-                send_two.at[k, peer[2]], recv_two.at[c, k], two_send.at[p, n], two_recv.at[k, code_of(d)], peer
-            )
-            copy.start()
-            sent.append(copy)
-        local = pltpu.make_async_copy(send_two.at[k, c], recv_two.at[c, k], local_sem.at[p])
-        local.start()
-        return sent, local
-
-    sent_a, local_a = finish_child(0)
+    def turn(source, k, slot):
+        wide[...] = source.astype(F32).reshape(size * blocks, size)
+        for j in range(blocks):
+            turned[k, slot, j] = wide[pl.ds(j, size, stride=blocks), :].astype(BF16)
+
+    def turn_own(s, carry):
+        slot = 2 * r + s
+        turn(child[f, rows_inv[f * 2 * grid + slot]], f, slot)
+        return carry
+
+    lax.fori_loop(0, 2, turn_own, 0)
 
     for copy in round_b:
         copy.wait_recv()
@@ -291,6 +248,59 @@
         copy.start()
         round_c.append(copy)
 
+    round_one = []
+    for n, (p, d) in enumerate(row_peers):
+        peer = row_at(p, d)
+        copy = remote(
+            send_one.at[peer[0], pl.ds(2 * peer[1], 2)],
+            recv_one.at[f, pl.ds(2 * r, 2)], one_send.at[n], one_recv.at[p, code_of(d)], peer,
+        )
+        copy.start()
+        round_one.append(copy)
+
+    for n, d in enumerate(row_steps):
+        source = pl.ds(pl.multiple_of(member(r, d, half, -1) * piece, 8), piece)
+        remote(sum_two, lead.at[source], lc_send.at[n], lc_recv.at[code_of(d)], row_at(0, d)).wait_recv()
+    factor_lead(lead, low_ref, inv_ref, work, size)
+    outs = [
+        pltpu.make_async_copy(low_ref, low_out, out_sem.at[0]),
+        pltpu.make_async_copy(inv_ref, inv_out, out_sem.at[1]),
+    ]
+
+    def finish_child(p):
+        k = f if p == 0 else other
+        for n, (q, d) in enumerate(row_peers):
+            if q != p:
+                continue
+            round_one[n].wait_recv()
+            source = member(r, d, half, -1)
+
+            def turn_one(s, carry):
+                turn(recv_one[k, 2 * source + s], k, 2 * source + s)
+                return carry
+
+            lax.fori_loop(0, 2, turn_one, 0)
+
+        def gather(j, carry):
+            row = row_slot[k * blocks + j]
+            for slot in range(2 * grid):
+                send_two[k, slot // 2, j, slot % 2] = turned[k, row, cols_inv[k * 2 * grid + slot]]
+            return carry
+
+        lax.fori_loop(0, blocks, gather, 0)
+        sent = []
+        for n, d in enumerate(col_steps):
+            peer = col_at(d)
+            copy = remote(
+                send_two.at[k, peer[2]], recv_two.at[c, k], two_send.at[p, n], two_recv.at[k, code_of(d)], peer
+            )
+            copy.start()
+            sent.append(copy)
+        local = pltpu.make_async_copy(send_two.at[k, c], recv_two.at[c, k], local_sem.at[p])
+        local.start()
+        return sent, local
+
+    sent_a, local_a = finish_child(0)
     sent_b, local_b = finish_child(1)
 
     for n in range(spots):
@@ -300,12 +310,12 @@
             fcol_ref[n - 1] = chunk[(n - 1) % 2, pl.ds(0, size, stride=spots), :]
     line(spots - 1, (spots - 1) % 2).wait()
     fcol_ref[spots - 1] = chunk[(spots - 1) % 2, pl.ds(0, size, stride=spots), :]
-
-    for n, d in enumerate(row_steps):
-        source = pl.ds(pl.multiple_of(member(r, d, half, -1) * piece, 8), piece)
-        remote(sum_two, lead.at[source], lc_send.at[n], lc_recv.at[code_of(d)], row_at(0, d)).wait_recv()
-    factor_lead(lead, low_ref, inv_ref, work, size)
-
+    outs.append(pltpu.make_async_copy(fcol_ref, fcol_out, out_sem.at[2]))
+    for copy in outs:
+        copy.start()
+
+    for copy in outs:
+        copy.wait()
     for copy in round_a + round_b + round_c + round_one:
         copy.wait_send()
     for sent, local, k in ((sent_a, local_a, f), (sent_b, local_b, other)):
@@ -321,7 +331,6 @@
     dma = pltpu.SemaphoreType.DMA
     smem = pl.BlockSpec(memory_space=SMEM)
     hbm = pl.BlockSpec(memory_space=HBM)
-    vmem = pl.BlockSpec(memory_space=VMEM)
     return pl.pallas_call(
         functools.partial(exchange_kernel, grid, size, blocks, spots),
         out_shape=[
@@ -331,8 +340,11 @@
             jax.ShapeDtypeStruct((spots, size, size), F32),
         ],
         in_specs=[smem] * 5 + [hbm] * 2,
-        out_specs=[hbm, vmem, vmem, vmem],
+        out_specs=[hbm] * 4,
         scratch_shapes=[
+            pltpu.VMEM((2, size, 2 * size), F32),
+            pltpu.VMEM((2 * size, 2 * size), F32),
+            pltpu.VMEM((spots, size, size), F32),
             pltpu.VMEM(child.shape, BF16),
             pltpu.VMEM((2, 2 * grid, size, blocks, size), BF16),
             pltpu.VMEM((2, 2 * grid, size, blocks, size), BF16),
@@ -350,6 +362,7 @@
             dma((2,)),
             dma((2,)),
             dma((2,)),
+            dma((3,)),
             dma((2 * grid,)),
             dma((2, grid)),
             dma((2, grid)),
@@ -381,10 +394,10 @@
 
 
 def spread_kernel(
-    grid, spots, size, row_ref, col_ref, child_hbm, flat_hbm, fcol_ref, low_ref, inv_ref,
-    whole_hbm, v_rows, rows_high, rows_low, cols_high, cols_low,
-    child, whole, rows_own, cols_own, rows_all, cols_all,
-    child_sem, in_sem, out_sem, one_send, one_recv, two_send, two_recv,
+    grid, spots, size, row_ref, col_ref, child_hbm, flat_hbm, fcol_hbm, low_hbm, inv_hbm,
+    whole_hbm, v_rows_out, rows_high_out, rows_low_out, cols_high_out, cols_low_out,
+    fcol_ref, low_ref, inv_ref, v_rows, rows_high, rows_low, cols_high, cols_low, child, whole, rows_own, cols_own, rows_all, cols_all,
+    child_sem, in_sem, out_sem, small_sem, v_sem, one_send, one_recv, two_send, two_recv,
 ):
     f, r, c = lax.axis_index("front"), lax.axis_index("row"), lax.axis_index("col")
     half = grid // 2
@@ -406,6 +419,12 @@
     line_in(0).start()
     for n in range(grid):
         pltpu.make_async_copy(child_hbm.at[n], child.at[n], child_sem.at[n]).start()
+    small = [
+        pltpu.make_async_copy(src, dst, small_sem.at[n])
+        for n, (src, dst) in enumerate(((fcol_hbm, fcol_ref), (low_hbm, low_ref), (inv_hbm, inv_ref)))
+    ]
+    for copy in small:
+        copy.start()
     for l in range(1, spots):
         line_in(l).start()
     meet([peer(lax.rem(me + d, grid)) for _, _, me, peer in groups for d in range(1, grid)])
@@ -420,6 +439,8 @@
         return parts
 
     line_in(0).wait()
+    for copy in small:
+        copy.wait()
     for n in range(grid):
         pltpu.make_async_copy(child_hbm.at[n], child.at[n], child_sem.at[n]).wait()
 
@@ -510,7 +531,7 @@
                 for n in range(1, half):
                     second(g, s, n, out.at[s]).start()
 
-    def solve(g, quarter):
+    def solve(g, quarter, n):
         out = groups[g][1]
 
         def one(i, carry):
@@ -527,9 +548,19 @@
             return carry
 
         lax.fori_loop(0, part, one, 0)
-
+        here = pl.ds(pl.multiple_of(quarter * part * size, size), part * size)
+        for i, (src, dst) in enumerate(factors[g]):
+            copy = pltpu.make_async_copy(src.at[here], dst.at[here], v_sem.at[g, n, i])
+            copy.start()
+            leaving.append(copy)
+
+    factors = (
+        ((rows_high, rows_high_out), (rows_low, rows_low_out), (v_rows, v_rows_out)),
+        ((cols_high, cols_high_out), (cols_low, cols_low_out)),
+    )
+    leaving = []
     for g in range(2):
-        solve(g, groups[g][2] // 2)
+        solve(g, groups[g][2] // 2, 0)
 
     for n in range(1, half):
         for g in range(2):
@@ -545,7 +576,7 @@
                     device_id=groups[g][3](lax.rem(me + 2 * n, grid)),
                     device_id_type=MESH,
                 ).wait_recv()
-            solve(g, quarter)
+            solve(g, quarter, n)
 
     for g in range(2):
         _, out, me, _ = groups[g]
@@ -560,6 +591,8 @@
                 second(g, s, n, out.at[s]).wait_send()
     for l in range(spots):
         line_out(l).wait()
+    for copy in leaving:
+        copy.wait()
 
 
 def spread(received, flat, fcol, low, inverse, row_pos, col_pos, grid):
@@ -569,14 +602,20 @@
     dma = pltpu.SemaphoreType.DMA
     smem = pl.BlockSpec(memory_space=SMEM)
     hbm = pl.BlockSpec(memory_space=HBM)
-    vmem = pl.BlockSpec(memory_space=VMEM)
     return pl.pallas_call(
         functools.partial(spread_kernel, grid, spots, size),
         out_shape=[jax.ShapeDtypeStruct(flat.shape, F32), jax.ShapeDtypeStruct((order, 2 * size), F32)]
         + [jax.ShapeDtypeStruct((order, 2 * size), BF16)] * 4,
-        in_specs=[smem] * 2 + [hbm] * 2 + [vmem] * 3,
-        out_specs=[hbm] + [vmem] * 5,
+        in_specs=[smem] * 2 + [hbm] * 5,
+        out_specs=[hbm] * 6,
         scratch_shapes=[
+            pltpu.VMEM(fcol.shape, F32),
+            pltpu.VMEM(low.shape, F32),
+            pltpu.VMEM(inverse.shape, F32),
+            pltpu.VMEM((order, 2 * size), F32),
+        ]
+        + [pltpu.VMEM((order, 2 * size), BF16)] * 4
+        + [
             pltpu.VMEM(received.shape, BF16),
             pltpu.VMEM(flat.shape, F32),
             pltpu.VMEM((spots, size, size), F32),
@@ -586,13 +625,15 @@
             dma((grid,)),
             dma((spots,)),
             dma((spots,)),
+            dma((3,)),
+            dma((2, half, 3)),
             dma((2, grid)),
             dma((2, 2)),
             dma((2, 2, half)),
             dma((2, 2, half)),
         ],
         compiler_params=pltpu.CompilerParams(
-            collective_id=3, has_side_effects=True, vmem_limit_bytes=48 * 2**20
+            collective_id=3, has_side_effects=True, vmem_limit_bytes=60 * 2**20
         ),
         cost_estimate=pl.CostEstimate(flops=40_000_000, bytes_accessed=8 * flat.size, transcendentals=0),
         name="spread",
@@ -640,7 +681,7 @@
             out_specs=line,
         ),
         out_shape=jax.ShapeDtypeStruct(whole.shape, F32),
-        compiler_params=pltpu.CompilerParams(dimension_semantics=("arbitrary",)),
+        compiler_params=pltpu.CompilerParams(dimension_semantics=("arbitrary",), vmem_limit_bytes=60 * 2**20),
         cost_estimate=pl.CostEstimate(flops=4_000_000_000, bytes_accessed=8 * whole.size, transcendentals=0),
         name="update",
     )(where, whole, v_rows, rows_high, rows_low, cols_high, cols_low)

time: 303 us -> 292 us (0.964)
  local copies, waits for them, and re-layouts: 12.8 us -> 6.17 us
    pallas_call x1, Pallas kernels: 217 us -> 208 us  [exchange(): pl.pallas_call(functools.partial(exchange_kernel, grid, size, blocks, spo...]
    unnamed x18 -> x2, local copies, waits for them, and re-layouts: 7.96 us -> 0.18 us
    pallas_call x1, Pallas kernels: 56.7 us -> 63.1 us  [spread(): pl.pallas_call(functools.partial(spread_kernel, grid, spots, size), out_s...]
where the time goes in v6:
time: 292 us
  Pallas kernels  283 us (97%)
  local copies, waits for them, and re-layouts  6.17 us (2%)
    pallas_call x1, Pallas kernels, exchange(): pl.pallas_call(functools.partial(exchange_kernel, grid, size, blocks, spo...  208 us
    pallas_call x1, Pallas kernels, spread(): pl.pallas_call(functools.partial(spread_kernel, grid, spots, size), out_s...  63.1 us
    pallas_call x1, Pallas kernels, update(): pl.pallas_call(functools.partial(update_kernel, spots, size), grid_spec=p...  12.6 us

profile of v6, /device:TPU:4, one launch (start us, length us, event | category | flops | bytes accessed | tf_op | source)
XLA Modules:
  0.0 291.5 jit_solution(14210270869139312344)
XLA Ops:
  0.0 0.6 pad_add_fusion.where_ref
  0.6 0.8 reshape.164
  1.4 0.1 convert_reduce_fusion
  1.6 0.3 dynamic-slice_reduce_fusion
  1.9 0.2 dynamic-slice_reduce_fusion.2
  2.1 0.1 reshape.170
  2.2 0.1 multiply_reduce_fusion
  2.3 0.1 select_reduce_fusion
  2.4 0.7 reshape.168.cols_inv
  3.1 0.1 fusion.5
  3.2 0.7 sub.34.lead_col
  3.9 0.1 eq.127
  3.9 0.1 reshape.165
  4.0 0.1 multiply_reduce_fusion.3
  4.2 0.7 reshape.167.row_slot
  4.9 0.6 sub.32.lead_row
  5.5 0.1 select_reduce_fusion.1
  5.6 0.6 reshape.166.rows_inv
  6.2 0.1 reshape.171
  6.2 0.5 multiply_reduce_fusion.1
  6.7 0.1 copy.40
  6.8 0.6 sub.30.col_ref
  7.5 0.1 copy.39
  7.6 0.6 sub.28.row_ref
  8.1 207.7 %exchange.1 = (bf16[8,2,8,2,128,128]{5,4,3,2,1,0:T(8,128)(2,1)}, f32[2,128,256]{2,1,0:T(8,128)}, f32[256,256]{1,0:T(8,128)}, f32[12,128,128]{2,1,0:T(8,128)}) custom-call(s32[32]{0:T(128)} %reshape.166.rows_inv, s32[16]{0:T(128)} %reshape.167.row_slot, s32[32]{0:T(128)} %reshape.168.cols_inv, s32[4]{0:T(128)} %sub.32.lead_row, s32[4]{0:T(128)} %sub.34.lead_col, ...), custom_call_target="tpu_custom_call" | custom-call | flops 400000000 | bytes 16777216 | tf_op jit(solution)/shard_map/exchange/pallas_call | solution.py:334
  215.8 63.1 %spread.1 = (f32[18432,128]{1,0:T(8,128)}, f32[1536,256]{1,0:T(8,128)}, bf16[1536,256]{1,0:T(8,128)(2,1)}, bf16[1536,256]{1,0:T(8,128)(2,1)}, bf16[1536,256]{1,0:T(8,128)(2,1)}, /*index=5*/bf16[1536,256]{1,0:T(8,128)(2,1)}) custom-call(s32[24]{0:T(128)} %sub.28.row_ref, s32[24]{0:T(128)} %sub.30.col_ref, ...), custom_call_target="tpu_custom_call" | custom-call | flops 40000000 | bytes 18874368 | tf_op jit(solution)/shard_map/spread/pallas_call | solution.py:605
  279.0 12.6 %update.1 = f32[18432,128]{1,0:T(8,128)} custom-call(s32[3]{0:T(128)} %pad_add_fusion.where_ref, f32[18432,128]{1,0:T(8,128)} %get-tuple-element.19.whole_ref, f32[1536,256]{1,0:T(8,128)} %get-tuple-element.20.v_rows, bf16[1536,256]{1,0:T(8,128)(2,1)} %get-tuple-element.21.rows_high, bf16[1536,256]{1,0:T(8,128)(2,1)} %get-tuple-element.22.rows_low, ...), custom_call_target="tpu_custom_call" | custom-call | flops 4000000000 | bytes 18874368 | tf_op jit(solution)/shard_map/update/pallas_call | solution.py:675
  (15 shorter events, 0.1 us)

commit v7 on v6

--- a/solution.py
+++ b/solution.py
@@ -17,49 +17,73 @@
 SMEM = pltpu.MemorySpace.SMEM
 
 
-def tables(maps, front, row, col, grid, parent_blocks):
+def table_kernel(grid, blocks, spots, maps, rows_inv, lead_row, lead_col, row_slot, cols_inv, row_pos, col_pos):
+    front, row, col = lax.axis_index("front"), lax.axis_index("row"), lax.axis_index("col")
+    total = blocks * grid
+    fills = ((rows_inv, 0), (row_slot, 0), (cols_inv, 0), (lead_row, -1), (lead_col, -1), (row_pos, -1), (col_pos, -1))
+    for ref, fill in fills:
+
+        def clear(i, carry, ref=ref, fill=fill):
+            ref[i] = fill
+            return carry
+
+        lax.fori_loop(0, ref.shape[0], clear, 0)
+
+    def order_of(values, q):
+        order = jnp.int32(0)
+        for before in range(q):
+            order = order + jnp.where(values[before] == values[q], 1, 0)
+        return order
+
+    def held(p, base, place, spare, inverse, lead):
+        blocks_at = [maps[base + q * grid + place] for q in range(blocks)]
+        target = [lax.rem(value, grid) for value in blocks_at]
+        for q in range(blocks):
+            if inverse is not None:
+                inverse[p * 2 * grid + 2 * target[q] + order_of(target, q)] = q
+            if lead is not None:
+                lead[jnp.where(blocks_at[q] < 2, 2 * p + blocks_at[q], spare)] = q
+
+    def one_pair(p, carry):
+        mine = (2 * p + front) * total
+        own = (2 * front + p) * total
+        held(p, mine, row, 4, rows_inv, lead_row)
+        held(p, mine, col, 4, None, lead_col)
+        held(p, own, col, 4, cols_inv, None)
+
+        def one_source(r, rank):
+            row_order, col_order = jnp.int32(0), jnp.int32(0)
+            for q in range(blocks):
+                value = maps[own + q * grid + r]
+                target, place = lax.rem(value, grid), lax.div(value, grid)
+                hit = target == row
+                row_slot[jnp.where(hit, p * blocks + rank, 2 * blocks)] = 2 * r + row_order
+                row_pos[jnp.where(hit, p * spots + place, 2 * spots)] = rank
+                row_order = row_order + jnp.where(hit, 1, 0)
+                rank = rank + jnp.where(hit, 1, 0)
+                hit = target == col
+                col_pos[jnp.where(hit, p * spots + place, 2 * spots)] = 2 * r + col_order
+                col_order = col_order + jnp.where(hit, 1, 0)
+            return rank
+
+        lax.fori_loop(0, grid, one_source, jnp.int32(0))
+        return carry
+
+    lax.fori_loop(0, 2, one_pair, 0)
+
+
+def tables(maps, grid, spots):
     blocks = maps.shape[-1] // grid
-    by_source = maps.reshape(2, 2, blocks, grid)
-    target = by_source % grid
-    place = by_source // grid
-    ids = jnp.arange(blocks, dtype=I32)
-    before = ids[None, :] < ids[:, None]
-    same = target[:, :, :, None, :] == target[:, :, None, :, :]
-    order = jnp.sum((same & before[None, None, :, :, None]).astype(I32), axis=3)
-    send_slot = target * 2 + order
-    recv_slot = jnp.arange(grid, dtype=I32) * 2 + order
-    mine = lax.dynamic_index_in_dim(by_source, front, 1, keepdims=False)
-    row_send = lax.dynamic_index_in_dim(
-        lax.dynamic_index_in_dim(send_slot, front, 1, keepdims=False), row, 2, keepdims=False
-    )
-    held_rows = lax.dynamic_index_in_dim(mine, row, 2, keepdims=False)
-    held_cols = lax.dynamic_index_in_dim(mine, col, 2, keepdims=False)
-    lead = jnp.arange(2, dtype=I32)
-    lead_row = jnp.sum(
-        (held_rows[:, None, :] == lead[None, :, None]).astype(I32) * (ids + 1), axis=-1
-    ) - 1
-    lead_col = jnp.sum(
-        (held_cols[:, None, :] == lead[None, :, None]).astype(I32) * (ids + 1), axis=-1
-    ) - 1
-    own = lambda value: lax.dynamic_index_in_dim(value, front, 0, keepdims=False)
-    own_target, own_place, own_recv = own(target), own(place), own(recv_slot)
-    col_send = lax.dynamic_index_in_dim(own(send_slot), col, 2, keepdims=False)
-    flat = lambda value: value.reshape(2, blocks * grid)
-    row_hit = flat(own_target == row).astype(I32)
-    col_hit = flat(own_target == col).astype(I32)
-    count = jnp.arange(blocks * grid, dtype=I32)
-    rank = jnp.sum(row_hit[:, None, :] * (count[None, :] < count[:, None]).astype(I32), axis=-1)
-    row_slot = jnp.sum(
-        row_hit[:, None, :] * (rank[:, None, :] == ids[None, :, None]).astype(I32) * flat(own_recv)[:, None, :],
-        axis=-1,
-    )
-    spots = jnp.arange(parent_blocks, dtype=I32)
-    at = (flat(own_place)[:, None, :] == spots[None, :, None]).astype(I32)
-    row_pos = jnp.sum(row_hit[:, None, :] * at * (rank + 1)[:, None, :], axis=-1) - 1
-    col_pos = jnp.sum(col_hit[:, None, :] * at * (flat(own_recv) + 1)[:, None, :], axis=-1) - 1
-    slots = jnp.arange(2 * grid, dtype=I32)
-    inverse = lambda sent: jnp.sum((sent[:, None, :] == slots[None, :, None]).astype(I32) * ids, axis=-1)
-    return inverse(row_send), lead_row, lead_col, row_slot, inverse(col_send), row_pos, col_pos
+    sizes = (4 * grid, 5, 5, 2 * blocks + 1, 4 * grid, 2 * spots + 1, 2 * spots + 1)
+    smem = pl.BlockSpec(memory_space=SMEM)
+    return pl.pallas_call(
+        functools.partial(table_kernel, grid, blocks, spots),
+        out_shape=[jax.ShapeDtypeStruct((size,), I32) for size in sizes],
+        in_specs=[smem],
+        out_specs=[smem] * len(sizes),
+        cost_estimate=pl.CostEstimate(flops=10_000, bytes_accessed=4096, transcendentals=0),
+        name="tables",
+    )(maps.reshape(-1))
 
 
 def meet(peers):
@@ -67,10 +91,6 @@
     for peer in peers:
         pl.semaphore_signal(barrier, inc=1, device_id=peer, device_id_type=MESH)
     pl.semaphore_wait(barrier, len(peers))
-
-
-def hop_order(grid):
-    return [d for pair in zip(range(1, grid), range(grid - 1, 0, -1)) for d in pair][: grid - 1]
 
 
 def codes(half, flip_cost):
@@ -397,7 +417,7 @@
     grid, spots, size, row_ref, col_ref, child_hbm, flat_hbm, fcol_hbm, low_hbm, inv_hbm,
     whole_hbm, v_rows_out, rows_high_out, rows_low_out, cols_high_out, cols_low_out,
     fcol_ref, low_ref, inv_ref, v_rows, rows_high, rows_low, cols_high, cols_low, child, whole, rows_own, cols_own, rows_all, cols_all,
-    child_sem, in_sem, out_sem, small_sem, v_sem, one_send, one_recv, two_send, two_recv,
+    child_sem, in_sem, out_sem, small_sem, v_sem, one_send, one_recv, flip_send, flip_recv, two_send, two_recv,
 ):
     f, r, c = lax.axis_index("front"), lax.axis_index("row"), lax.axis_index("col")
     half = grid // 2
@@ -405,7 +425,6 @@
     row_peer = lambda i: (f, r, i)
     col_peer = lambda i: (f, i, c)
     groups = ((rows_own, rows_all, c, row_peer), (cols_own, cols_all, r, col_peer))
-    order = hop_order(grid)
 
     def line(l):
         return pl.ds(pl.multiple_of(l * size * spots, size * spots), size * spots)
@@ -457,48 +476,34 @@
         for j in range(spots):
             cols_own[j] = added(whole[pl.ds(j, size, stride=spots), :], from_child(0, j)).T
 
-    def first(g, s, n):
+    def remote(src, dst, send_sem, recv_sem, peer):
+        return pltpu.make_async_remote_copy(
+            src_ref=src, dst_ref=dst, send_sem=send_sem, recv_sem=recv_sem, device_id=peer, device_id_type=MESH
+        )
+
+    def first(g, n):
         source, out, me, peer = groups[g]
-        to = lax.rem(s + n, grid)
-        piece = pl.ds((to // 2) * part, part)
-        return pltpu.make_async_remote_copy(
-            src_ref=source.at[piece],
-            dst_ref=out.at[s, piece],
-            send_sem=one_send.at[g, n],
-            recv_sem=one_recv.at[g, s],
-            device_id=peer(to),
-            device_id_type=MESH,
-        )
-
-    def second(g, s, n, source):
+        piece = pl.ds(n * part, part)
+        to = peer(2 * n + lax.rem(me, 2))
+        return remote(source.at[piece], out.at[lax.rem(me, 2), piece], one_send.at[g, n], one_recv.at[g], to)
+
+    def piece_of(g):
+        return pl.ds((groups[g][2] // 2) * part, part)
+
+    def panel_of(g, t):
+        return lax.rem(groups[g][2] + t, 2)
+
+    def across(g, source):
         _, out, me, peer = groups[g]
-        piece = pl.ds((me // 2) * part, part)
-        return pltpu.make_async_remote_copy(
-            src_ref=source.at[piece],
-            dst_ref=out.at[s, piece],
-            send_sem=two_send.at[g, s, n],
-            recv_sem=two_recv.at[g, s, n],
-            device_id=peer(lax.rem(me + 2 * n, grid)),
-            device_id_type=MESH,
-        )
-
-    for g in range(2):
-        for s in range(2):
-
-            @pl.when(groups[g][2] == s)
-            def _():
-                for n in order:
-                    first(g, s, n).start()
-
-    for g in range(2):
-        source, out, me, _ = groups[g]
-        for s in range(2):
-
-            @pl.when(me == s)
-            def _():
-                out[s, pl.ds(0, part)] = source[pl.ds(0, part)]
-                for n in range(1, half):
-                    second(g, s, n, source).start()
+        to = peer(2 * (me // 2) + lax.rem(me + 1, 2))
+        piece = piece_of(g)
+        return remote(source.at[piece], out.at[panel_of(g, 0), piece], flip_send.at[g], flip_recv.at[g], to)
+
+    def along(g, t, n, source):
+        _, out, me, peer = groups[g]
+        piece = piece_of(g)
+        to = peer(lax.rem(me + 2 * n, grid))
+        return remote(source.at[piece], out.at[panel_of(g, t), piece], two_send.at[g, t, n], two_recv.at[g, t, n], to)
 
     def assemble(l, carry):
         @pl.when(l > 0)
@@ -511,25 +516,48 @@
         line_out(l).start()
         return carry
 
-    lax.fori_loop(0, spots, assemble, 0)
+    cuts = [spots * n // 3 for n in range(4)]
 
     for g in range(2):
-        _, out, me, _ = groups[g]
-        for s in range(2):
-
-            @pl.when(me != s)
-            def _():
-                piece = pl.ds((me // 2) * part, part)
-                pltpu.make_async_remote_copy(
-                    src_ref=out.at[s, piece],
-                    dst_ref=out.at[s, piece],
-                    send_sem=one_send.at[g, 0],
-                    recv_sem=one_recv.at[g, s],
-                    device_id=groups[g][3](s),
-                    device_id_type=MESH,
-                ).wait_recv()
-                for n in range(1, half):
-                    second(g, s, n, out.at[s]).start()
+
+        @pl.when(groups[g][2] < 2)
+        def _():
+            source, out, me, _ = groups[g]
+            for n in range(1, half):
+                first(g, n).start()
+            across(g, source).start()
+            for n in range(1, half):
+                along(g, 0, n, source).start()
+            out[me, pl.ds(0, part)] = source[pl.ds(0, part)]
+
+    lax.fori_loop(cuts[0], cuts[1], assemble, 0)
+
+    for g in range(2):
+
+        @pl.when(groups[g][2] >= 2)
+        def _():
+            here = groups[g][1].at[panel_of(g, 0)]
+            remote(
+                here.at[piece_of(g)], here.at[piece_of(g)], one_send.at[g, 0], one_recv.at[g],
+                groups[g][3](lax.rem(groups[g][2], 2)),
+            ).wait_recv()
+            across(g, here).start()
+            for n in range(1, half):
+                along(g, 0, n, here).start()
+
+    lax.fori_loop(cuts[1], cuts[2], assemble, 0)
+
+    for g in range(2):
+        here = groups[g][1].at[panel_of(g, 1)]
+        me = groups[g][2]
+        remote(
+            here.at[piece_of(g)], here.at[piece_of(g)], flip_send.at[g], flip_recv.at[g],
+            groups[g][3](2 * (me // 2) + lax.rem(me + 1, 2)),
+        ).wait_recv()
+        for n in range(1, half):
+            along(g, 1, n, here).start()
+
+    lax.fori_loop(cuts[2], cuts[3], assemble, 0)
 
     def solve(g, quarter, n):
         out = groups[g][1]
@@ -567,28 +595,24 @@
             source, out, me, _ = groups[g]
             quarter = lax.rem(me // 2 + half - n, half)
             piece = pl.ds(quarter * part, part)
-            for s in range(2):
-                pltpu.make_async_remote_copy(
-                    src_ref=out.at[s, piece],
-                    dst_ref=out.at[s, piece],
-                    send_sem=two_send.at[g, s, n],
-                    recv_sem=two_recv.at[g, s, n],
-                    device_id=groups[g][3](lax.rem(me + 2 * n, grid)),
-                    device_id_type=MESH,
-                ).wait_recv()
+            for t in range(2):
+                here = out.at[panel_of(g, t), piece]
+                to = groups[g][3](lax.rem(me + 2 * n, grid))
+                remote(here, here, two_send.at[g, t, n], two_recv.at[g, t, n], to).wait_recv()
             solve(g, quarter, n)
 
     for g in range(2):
-        _, out, me, _ = groups[g]
-        for s in range(2):
-
-            @pl.when(me == s)
-            def _():
-                for n in order:
-                    first(g, s, n).wait_send()
-
+        here = groups[g][1].at[0]
+
+        @pl.when(groups[g][2] < 2)
+        def _():
             for n in range(1, half):
-                second(g, s, n, out.at[s]).wait_send()
+                first(g, n).wait_send()
+
+        across(g, here).wait_send()
+        for t in range(2):
+            for n in range(1, half):
+                along(g, t, n, here).wait_send()
     for l in range(spots):
         line_out(l).wait()
     for copy in leaving:
@@ -627,8 +651,10 @@
             dma((spots,)),
             dma((3,)),
             dma((2, half, 3)),
-            dma((2, grid)),
-            dma((2, 2)),
+            dma((2, half)),
+            dma((2,)),
+            dma((2,)),
+            dma((2,)),
             dma((2, 2, half)),
             dma((2, 2, half)),
         ],
@@ -693,9 +719,7 @@
     spots, size, _, _ = local.shape
     flat = local.reshape(spots * size * spots, size)
     child = child_updates[0, :, :, 0, :, :, 0, :]
-    rows_inv, lead_row, lead_col, row_slot, cols_inv, row_pos, col_pos = tables(
-        index_maps, front, row, col, grid, spots
-    )
+    rows_inv, lead_row, lead_col, row_slot, cols_inv, row_pos, col_pos = tables(index_maps, grid, spots)
     where = jnp.stack([front, row, col]).astype(I32)
     received, low, inverse, fcol = exchange(
         child, flat, rows_inv, row_slot, cols_inv, lead_row, lead_col, grid, spots

time: 292 us -> 281 us (0.962)
  Pallas kernels: 283 us -> 278 us
  local copies, waits for them, and re-layouts: 6.17 us -> 1.32 us
    pallas_call x1, Pallas kernels: 63.1 us -> 53.9 us  [spread(): pl.pallas_call(functools.partial(spread_kernel, grid, spots, size), out_s...]
    pallas_call x0 -> x1, Pallas kernels: none -> 3.72 us  [tables(): pl.pallas_call(functools.partial(table_kernel, grid, blocks, spots), out_...]
where the time goes in v7:
time: 281 us; the launch traced here: 280 us
  Pallas kernels  278 us (99%)
    pallas_call x1, Pallas kernels, exchange(): pl.pallas_call(functools.partial(exchange_kernel, grid, size, blocks, spo...  208 us
    pallas_call x1, Pallas kernels, spread(): pl.pallas_call(functools.partial(spread_kernel, grid, spots, size), out_s...  53.9 us
    pallas_call x1, Pallas kernels, update(): pl.pallas_call(functools.partial(update_kernel, spots, size), grid_spec=p...  12.6 us

profile of v7, /device:TPU:4, one launch (start us, length us, event | category | flops | bytes accessed | tf_op | source)
XLA Modules:
  0.0 279.8 jit_solution(8926390024352586004)
XLA Ops:
  0.0 1.3 reshape.6.maps
  1.3 3.7 %tables.1 = (s32[32]{0:T(128)}, s32[5]{0:T(128)}, s32[5]{0:T(128)}, s32[17]{0:T(128)}, s32[32]{0:T(128)}, /*index=5*/s32[25]{0:T(128)}, s32[25]{0:T(128)}) custom-call(s32[256]{0:T(256)} %reshape.6.maps), custom_call_target="tpu_custom_call" | custom-call | flops 10000 | bytes 4096 | tf_op jit(solution)/shard_map/tables/pallas_call | solution.py:79
  5.0 207.7 %exchange.1 = (bf16[8,2,8,2,128,128]{5,4,3,2,1,0:T(8,128)(2,1)}, f32[2,128,256]{2,1,0:T(8,128)}, f32[256,256]{1,0:T(8,128)}, f32[12,128,128]{2,1,0:T(8,128)}) custom-call(s32[32]{0:T(128)} %get-tuple-element.24.rows_inv, s32[17]{0:T(128)} %get-tuple-element.25.row_slot, s32[32]{0:T(128)} %get-tuple-element.26.cols_inv, s32[5]{0:T(128)} %get-tuple-element.27.lead_row, ...), custom_call_target="tpu_custom_call" | custom-call | flops 400000000 | bytes 16777216 | tf_op jit(solution)/shard_map/exchange/pallas_call | solution.py:354
  212.8 53.9 %spread.1 = (f32[18432,128]{1,0:T(8,128)}, f32[1536,256]{1,0:T(8,128)}, bf16[1536,256]{1,0:T(8,128)(2,1)}, bf16[1536,256]{1,0:T(8,128)(2,1)}, bf16[1536,256]{1,0:T(8,128)(2,1)}, /*index=5*/bf16[1536,256]{1,0:T(8,128)(2,1)}) custom-call(s32[25]{0:T(128)} %get-tuple-element.22.row_ref, s32[25]{0:T(128)} %get-tuple-element.23.col_ref, ...), custom_call_target="tpu_custom_call" | custom-call | flops 40000000 | bytes 18874368 | tf_op jit(solution)/shard_map/spread/pallas_call | solution.py:629
  266.7 0.6 pad_add_fusion.where_ref
  267.3 12.6 %update.1 = f32[18432,128]{1,0:T(8,128)} custom-call(s32[3]{0:T(128)} %pad_add_fusion.where_ref, f32[18432,128]{1,0:T(8,128)} %get-tuple-element.33.whole_ref, f32[1536,256]{1,0:T(8,128)} %get-tuple-element.34.v_rows, bf16[1536,256]{1,0:T(8,128)(2,1)} %get-tuple-element.35.rows_high, bf16[1536,256]{1,0:T(8,128)(2,1)} %get-tuple-element.36.rows_low, ...), custom_call_target="tpu_custom_call" | custom-call | flops 4000000000 | bytes 18874368 | tf_op jit(solution)/shard_map/update/pallas_call | solution.py:701

commit v8 on v7

--- a/solution.py
+++ b/solution.py
@@ -19,7 +19,6 @@
 
 def table_kernel(grid, blocks, spots, maps, rows_inv, lead_row, lead_col, row_slot, cols_inv, row_pos, col_pos):
     front, row, col = lax.axis_index("front"), lax.axis_index("row"), lax.axis_index("col")
-    total = blocks * grid
     fills = ((rows_inv, 0), (row_slot, 0), (cols_inv, 0), (lead_row, -1), (lead_col, -1), (row_pos, -1), (col_pos, -1))
     for ref, fill in fills:
 
@@ -36,7 +35,7 @@
         return order
 
     def held(p, base, place, spare, inverse, lead):
-        blocks_at = [maps[base + q * grid + place] for q in range(blocks)]
+        blocks_at = [maps[base[0], base[1], q * grid + place] for q in range(blocks)]
         target = [lax.rem(value, grid) for value in blocks_at]
         for q in range(blocks):
             if inverse is not None:
@@ -45,8 +44,7 @@
                 lead[jnp.where(blocks_at[q] < 2, 2 * p + blocks_at[q], spare)] = q
 
     def one_pair(p, carry):
-        mine = (2 * p + front) * total
-        own = (2 * front + p) * total
+        mine, own = (p, front), (front, p)
         held(p, mine, row, 4, rows_inv, lead_row)
         held(p, mine, col, 4, None, lead_col)
         held(p, own, col, 4, cols_inv, None)
@@ -54,7 +52,7 @@
         def one_source(r, rank):
             row_order, col_order = jnp.int32(0), jnp.int32(0)
             for q in range(blocks):
-                value = maps[own + q * grid + r]
+                value = maps[front, p, q * grid + r]
                 target, place = lax.rem(value, grid), lax.div(value, grid)
                 hit = target == row
                 row_slot[jnp.where(hit, p * blocks + rank, 2 * blocks)] = 2 * r + row_order
@@ -83,7 +81,7 @@
         out_specs=[smem] * len(sizes),
         cost_estimate=pl.CostEstimate(flops=10_000, bytes_accessed=4096, transcendentals=0),
         name="tables",
-    )(maps.reshape(-1))
+    )(maps)
 
 
 def meet(peers):
@@ -675,11 +673,11 @@
     def dot(a, b):
         return lax.dot_general(a, b, (((1,), (1,)), ((), ())), preferred_element_type=F32)
 
-    high, low = rows_high[...], rows_low[...]
+    left = jnp.concatenate([rows_high[...], rows_high[...], rows_low[...]], axis=1)
     for j in range(0, spots, wide):
         there = pl.ds(j * size, wide * size)
         ch, cl = cols_high[there, :], cols_low[there, :]
-        product = dot(high, ch) + (dot(high, cl) + dot(low, ch))
+        product = dot(left, jnp.concatenate([ch, cl, ch], axis=1))
         for i in range(count):
             top = (step == 0) & (my_row < 2) & (i == 0)
             for w in range(wide):

time: 281 us -> 279 us (level)
  no operation moved by 1% of the time
where the time goes in v8:
time: 279 us
  Pallas kernels  278 us (100%)
    pallas_call x1, Pallas kernels, exchange(): pl.pallas_call(functools.partial(exchange_kernel, grid, size, blocks, spo...  208 us
    pallas_call x1, Pallas kernels, spread(): pl.pallas_call(functools.partial(spread_kernel, grid, spots, size), out_s...  53.9 us
    pallas_call x1, Pallas kernels, update(): pl.pallas_call(functools.partial(update_kernel, spots, size), grid_spec=p...  12.5 us

profile of v8, /device:TPU:4, one launch (start us, length us, event | category | flops | bytes accessed | tf_op | source)
XLA Modules:
  0.0 278.8 jit_solution(3145326039424836115)
XLA Ops:
  0.0 3.9 %tables.1 = (s32[32]{0:T(128)}, s32[5]{0:T(128)}, s32[5]{0:T(128)}, s32[17]{0:T(128)}, s32[32]{0:T(128)}, /*index=5*/s32[25]{0:T(128)}, s32[25]{0:T(128)}) custom-call(s32[2,2,64]{2,1,0:T(2,128)} %maps.1), custom_call_target="tpu_custom_call" | custom-call | flops 10000 | bytes 4096 | tf_op jit(solution)/shard_map/tables/pallas_call | solution.py:77
  3.9 207.7 %exchange.1 = (bf16[8,2,8,2,128,128]{5,4,3,2,1,0:T(8,128)(2,1)}, f32[2,128,256]{2,1,0:T(8,128)}, f32[256,256]{1,0:T(8,128)}, f32[12,128,128]{2,1,0:T(8,128)}) custom-call(s32[32]{0:T(128)} %get-tuple-element.24.rows_inv, s32[17]{0:T(128)} %get-tuple-element.25.row_slot, s32[32]{0:T(128)} %get-tuple-element.26.cols_inv, s32[5]{0:T(128)} %get-tuple-element.27.lead_row, ...), custom_call_target="tpu_custom_call" | custom-call | flops 400000000 | bytes 16777216 | tf_op jit(solution)/shard_map/exchange/pallas_call | solution.py:352
  211.7 53.9 %spread.1 = (f32[18432,128]{1,0:T(8,128)}, f32[1536,256]{1,0:T(8,128)}, bf16[1536,256]{1,0:T(8,128)(2,1)}, bf16[1536,256]{1,0:T(8,128)(2,1)}, bf16[1536,256]{1,0:T(8,128)(2,1)}, /*index=5*/bf16[1536,256]{1,0:T(8,128)(2,1)}) custom-call(s32[25]{0:T(128)} %get-tuple-element.22.row_ref, s32[25]{0:T(128)} %get-tuple-element.23.col_ref, ...), custom_call_target="tpu_custom_call" | custom-call | flops 40000000 | bytes 18874368 | tf_op jit(solution)/shard_map/spread/pallas_call | solution.py:627
  265.6 0.7 pad_add_fusion.where_ref
  266.2 12.5 %update.1 = f32[18432,128]{1,0:T(8,128)} custom-call(s32[3]{0:T(128)} %pad_add_fusion.where_ref, f32[18432,128]{1,0:T(8,128)} %get-tuple-element.33.whole_ref, f32[1536,256]{1,0:T(8,128)} %get-tuple-element.34.v_rows, bf16[1536,256]{1,0:T(8,128)(2,1)} %get-tuple-element.35.rows_high, bf16[1536,256]{1,0:T(8,128)(2,1)} %get-tuple-element.36.rows_low, ...), custom_call_target="tpu_custom_call" | custom-call | flops 4000000000 | bytes 18874368 | tf_op jit(solution)/shard_map/update/pallas_call | solution.py:699
